TPU v7x, 256 devices: a whole 4x4x8 slice. The times are simulated.
256 devices in a mesh: mkt: 32 (over z, x_lo, core), draw: 4 (over y), nest: 2 (over x_hi).
Axes of the slice: x: 4 (x_hi: 2, x_lo: 2; x = x_hi * 2 + x_lo), y: 4, z: 8, core: 2. Of those that a mesh axis runs over, the one named last changes fastest.
Arguments:
- features: bfloat16 [32, 512, 1024], P(None, 'mkt'), may hold values from -1.5 to 1.5
- taste_draws: bfloat16 [1024, 32, 512], P('mkt', None, 'draw'), may hold values from -4 to 4
- taste_scale: float32 [32], replicated, may hold values from 0.2 to 1
- nest_param: float32 [16], P('nest'), may hold values from 0.3 to 0.95
- members: int32 [16, 48], P('nest'), may hold values from -1 to 511, as said below
- log_share: float32 [512, 1024], P('mkt'), may hold values from -10 to -7
Outputs:
- mean_utility: float32 [1024, 768], P('mkt', 'nest')
- model_share: float32 [1024, 768], P('mkt', 'nest')
Inputs may be any that keep to these rules, and one draw needn't show every extreme that they name: `members`: every product id 0 to 511 stands in exactly one slot; in each nest's row the ids fill the first slots and -1 fills the rest; each nest holds at least 16 products, and some nest fills all 48 slots.
All inputs are finite; a program needn't handle non-finite values.
Results may differ from a plain program's by a relative error of at most 0.0013.
The roundings to bfloat16 on the way count: a program that leaves them out, or rounds other values in their place, can miss the bound.
Values may be sent and summed in bfloat16 or wider, within the bound.
No kernel may reach another device: no remote copies, remote signals or barrier semaphores. Data moves between devices by JAX's collectives and lax.ppermute only.
A program may use at most 64 MiB of HBM per device.

v0:
```python
import jax
import jax.numpy as jnp
from jax import lax
from jax.sharding import PartitionSpec as P

ITERS = 3


def copy_for_each(value, axis):
    copies = jnp.broadcast_to(value, (lax.axis_size(axis), *value.shape))
    return lax.all_to_all(copies, axis, split_axis=0, concat_axis=0, tiled=True)


def in_order(pieces, dim):
    dims = list(pieces.shape[1:])
    dims[dim] *= pieces.shape[0]
    return jnp.moveaxis(pieces, 0, dim).reshape(dims)


def collect(value, axis, dim):
    pieces = copy_for_each(value, axis)
    return in_order(pieces, dim)


def over_pieces(value, axis):
    pieces = lax.all_gather(value, axis)
    return pieces.sum(axis=0)


def of_everyone(value, axis):
    return copy_for_each(value, axis).sum(axis=0)


def revise(value_slot, slot_share, target, nest_rate, occupied):
    safe_share = jnp.where(occupied[None, :], slot_share, 1.0)
    moved_value = value_slot + (1.0 - nest_rate)[None, :] * (target - jnp.log(safe_share))
    return jnp.where(occupied[None, :], moved_value, 0.0)


def shards(features, taste_draws, taste_scale, nest_param, members, log_share):
    groups = lax.axis_size(("draw", "nest"))
    part_width = features.shape[0] // groups
    offset = lax.axis_index(("draw", "nest")) * part_width
    portion = lax.dynamic_slice_in_dim(features, offset, part_width, 0)
    moved_part = lax.all_to_all(portion, "mkt", split_axis=2, concat_axis=1, tiled=True)
    market_x = collect(moved_part, ("draw", "nest"), 0)
    market_log = lax.all_to_all(log_share, "mkt", split_axis=1, concat_axis=0, tiled=True)
    market_list = market_log.shape[1]
    product_count = market_log.shape[0]
    nest_count = members.shape[0]
    slot_count = members.shape[1]
    columns = nest_count * slot_count
    draws_here = taste_draws.shape[2]
    total_draws = draws_here * lax.axis_size("draw")
    product_ids = members.reshape(columns)
    occupied = product_ids >= 0
    safe_ids = jnp.maximum(product_ids, 0)
    live_flag = occupied.astype(jnp.float32)
    product_range = jnp.arange(product_count, dtype=jnp.int32)
    onehot = ((safe_ids[None, :] == product_range[:, None]) & occupied[None, :]).astype(
        jnp.bfloat16
    )
    slot_features = jnp.einsum(
        "kjm,js->mks", market_x, onehot, preferred_element_type=jnp.float32
    ).astype(jnp.bfloat16)
    slot_log = jnp.transpose(jnp.take(market_log, safe_ids, axis=0), (1, 0))
    outside = 1.0 - jnp.sum(jnp.exp(market_log), axis=0)
    value_slot = jnp.where(occupied[None, :], slot_log - jnp.log(outside)[:, None], 0.0)
    taste_matrix = (taste_scale[None, :, None] * taste_draws.astype(jnp.float32)).astype(
        jnp.bfloat16
    )
    nest_rate = jnp.repeat(nest_param, slot_count)
    mean_utility_part = jnp.einsum(
        "dve,dvb->deb", slot_features, taste_matrix, preferred_element_type=jnp.float32
    )
    slot_share = jnp.zeros_like(value_slot)
    for iteration in range(ITERS):
        utility = live_flag[None, :, None] * jnp.exp(
            (value_slot[:, :, None] + mean_utility_part) / nest_rate[None, :, None]
        )
        grouped = utility.reshape(market_list, nest_count, slot_count, draws_here)
        inner_sum = jnp.sum(grouped, axis=2)
        inclusive_value = jnp.exp(nest_param[None, :, None] * jnp.log(inner_sum))
        totals = over_pieces(jnp.sum(inclusive_value, axis=1), "nest")
        nest_ratio = inclusive_value / (inner_sum * (1.0 + totals)[:, None, :])
        share_terms = jnp.sum(grouped * nest_ratio[:, :, None, :], axis=3).reshape(
            market_list, columns
        )
        slot_share = of_everyone(share_terms, "draw") / total_draws
        value_slot = revise(value_slot, slot_share, slot_log, nest_rate, occupied)
    return (value_slot, slot_share)


def solution(mesh):
    in_specs = (
        P(None, "mkt", None),
        P("mkt", None, "draw"),
        P(),
        P("nest"),
        P("nest", None),
        P("mkt", None),
    )
    out_specs = (P("mkt", "nest"), P("mkt", "nest"))
    return jax.shard_map(shards, mesh=mesh, in_specs=in_specs, out_specs=out_specs, check_vma=False)
```

profile of v0, /device:TPU:2, one launch (start us, length us, event | category | flops | bytes accessed | tf_op | source)
XLA Modules:
  0.0 173.7 jit_solution(3801479404405537700)
XLA Ops:
  0.7 1.2 copy-done
  2.6 1.8 %reshape.136 = bf16[32,2,1024]{2,1,0:T(2,128)(2,1)} reshape(bf16[1024,4,16]{2,1,0:T(4,128)(2,1)S(1)} %bitcast.73) | data formatting | bytes 262144
  4.4 10.1 %all-to-all-start.1 = ((bf16[32,2,1024]{2,1,0:T(2,128)(2,1)}), bf16[32,2,1024]{2,1,0:T(2,128)(2,1)S(1)}, u32[]{:S(2)}, u32[]{:S(2)}) async-start(bf16[32,2,1024]{2,1,0:T(2,128)(2,1)} %reshape.136), calls=%async_computation.1 | async-start | bytes 262144 | tf_op jit(solution)/shard_map/all_to_all | solution.py:45
  14.5 1.0 all_to_all.39
  15.6 0.8 reshape.138
  16.4 7.3 %all-to-all-done.1 = bf16[32,2,1024]{2,1,0:T(2,128)(2,1)S(1)} async-done(((bf16[32,2,1024]{2,1,0:T(2,128)(2,1)}), bf16[32,2,1024]{2,1,0:T(2,128)(2,1)S(1)}, u32[]{:S(2)}, u32[]{:S(2)}) %all-to-all-start.1) | async-done | bytes 131104 | tf_op jit(solution)/shard_map/all_to_all | solution.py:45
  23.7 3.9 %all-to-all-start = ((f32[32,1,512]{2,1,0:T(1,128)}), f32[32,1,512]{2,1,0:T(1,128)S(1)}, u32[]{:S(2)}, u32[]{:S(2)}) async-start(f32[32,1,512]{2,1,0:T(1,128)} %reshape.138), calls=%async_computation | async-start | bytes 131072 | tf_op jit(solution)/shard_map/all_to_all | solution.py:47
  29.9 5.6 %all-to-all-done = f32[32,1,512]{2,1,0:T(1,128)S(1)} async-done(((f32[32,1,512]{2,1,0:T(1,128)}), f32[32,1,512]{2,1,0:T(1,128)S(1)}, u32[]{:S(2)}, u32[]{:S(2)}) %all-to-all-start) | async-done | bytes 65568 | tf_op jit(solution)/shard_map/all_to_all | solution.py:47
  35.6 1.1 broadcast_in_dim.98
  36.7 6.0 %all-to-all-start.2 = ((bf16[8,4,512,32]{2,3,1,0:T(8,128)(2,1)}), bf16[8,4,512,32]{2,3,1,0:T(8,128)(2,1)S(1)}, u32[]{:S(2)}, u32[]{:S(2)}) async-start(bf16[8,4,512,32]{2,3,1,0:T(8,128)(2,1)} %broadcast_in_dim.98), calls=%async_computation.2 | async-start | bytes 2097152 | tf_op jit(solution)/shard_map/all_to_all | solution.py:11
  43.6 0.8 reduce.4
  44.5 1.1 gather_fusion
  46.0 13.7 %all-to-all-done.2 = bf16[8,4,512,32]{2,3,1,0:T(8,128)(2,1)S(1)} async-done(((bf16[8,4,512,32]{2,3,1,0:T(8,128)(2,1)}), bf16[8,4,512,32]{2,3,1,0:T(8,128)(2,1)S(1)}, u32[]{:S(2)}, u32[]{:S(2)}) %all-to-all-start.2) | async-done | bytes 1048608 | tf_op jit(solution)/shard_map/all_to_all | solution.py:11
  59.7 6.8 %exponential_multiply_fusion.2 = (f32[32,384,128]{2,1,0:T(8,128)}, f32[32,384,128]{2,1,0:T(8,128)}) fusion(f32[384]{0:T(512)S(1)} %reshape.118, f32[32,384]{1,0:T(8,128)S(1)} %copy.32, f32[384]{0:T(512)S(1)} %convert_element_type.20, bf16[32,32,128]{2,1,0:T(8,128)(2,1)S(1)} %copy-done.3, f32[32]{0:T(128)S(1)} %copy-done.4, ...), kind=kOutput, calls=%fused_computation.6 | convolution fusion | flops 509214720 | bytes 13947904 | tf_op jit(solution)/shard_map/dve,dvb->deb/dot_general | solution.py:73
  66.6 3.7 %reduce_sum.145 = f32[32,8,128]{2,1,0:T(8,128)S(1)} reduce(f32[32,8,48,128]{3,2,1,0:T(8,128)} %bitcast.69, f32[]{:T(128)} %constant.18.clone.1), dimensions={2}, to_apply=%region_1.2 | reduce | flops 1540096 | bytes 6422532 | tf_op jit(solution)/shard_map/reduce_sum | solution.py:82
  70.3 5.9 %all-gather = f32[64,128]{1,0:T(8,128)S(1)} all-gather(f32[32,128]{1,0:T(8,128)S(1)} %fusion.26), channel_id=2, replica_groups=mesh['mkt'=32,'draw'=4,'nest'=2] {'nest'}, dimensions={0}, use_global_device_ids=true | all-gather | bytes 49152 | tf_op jit(solution)/shard_map/all_gather | solution.py:26
  76.4 6.2 %bitcast_multiply_fusion.2 = f32[32,384,128]{2,1,0:T(8,128)} fusion(f32[32,384,128]{2,1,0:T(8,128)} %get-tuple-element.12, f32[32,8,128]{2,1,0:T(8,128)S(1)} %multiply_divide_fusion.2), kind=kLoop, calls=%fused_computation.3 | loop fusion | flops 1572864 | bytes 12713984 | tf_op jit(solution)/shard_map/mul | solution.py:86
  82.6 4.5 %reduce_sum.148 = f32[32,384]{1,0:T(8,128)S(1)} reduce(f32[32,384,128]{2,1,0:T(8,128)} %bitcast_multiply_fusion.2, f32[]{:T(128)} %constant.18.clone.1), dimensions={2}, to_apply=%region_4.5 | reduce | flops 1560576 | bytes 6340612 | tf_op jit(solution)/shard_map/reduce_sum | solution.py:86
  87.7 3.5 %all-to-all-start.3 = ((f32[4,32,384]{2,1,0:T(8,128)}), f32[4,32,384]{2,1,0:T(8,128)S(1)}, u32[]{:S(2)}, u32[]{:S(2)}) async-start(f32[4,32,384]{2,1,0:T(8,128)} %broadcast_in_dim.99), calls=%async_computation.3 | async-start | bytes 393216 | tf_op jit(solution)/shard_map/all_to_all | solution.py:11
  91.3 6.1 %all-to-all-done.3 = f32[4,32,384]{2,1,0:T(8,128)S(1)} async-done(((f32[4,32,384]{2,1,0:T(8,128)}), f32[4,32,384]{2,1,0:T(8,128)S(1)}, u32[]{:S(2)}, u32[]{:S(2)}) %all-to-all-start.3) | async-done | bytes 196640 | tf_op jit(solution)/shard_map/all_to_all | solution.py:11
  97.9 6.8 %exponential_multiply_fusion.1 = f32[32,384,128]{2,1,0:T(8,128)} fusion(f32[32,384,128]{2,1,0:T(8,128)} %get-tuple-element.13, f32[32,384]{1,0:T(8,128)S(1)} %copy.38, f32[384]{0:T(512)S(1)} %reshape.118, f32[384]{0:T(512)S(1)} %convert_element_type.20), kind=kLoop, calls=%fused_computation.5 | loop fusion | flops 4718592 | bytes 12635136 | tf_op jit(solution)/shard_map/mul | solution.py:78
  104.7 3.7 %reduce_sum.150 = f32[32,8,128]{2,1,0:T(8,128)S(1)} reduce(f32[32,8,48,128]{3,2,1,0:T(8,128)} %bitcast.70, f32[]{:T(128)} %constant.18.clone.1), dimensions={2}, to_apply=%region_6.7 | reduce | flops 1540096 | bytes 6422532 | tf_op jit(solution)/shard_map/reduce_sum | solution.py:82
  108.5 5.9 %all-gather.1 = f32[64,128]{1,0:T(8,128)S(1)} all-gather(f32[32,128]{1,0:T(8,128)S(1)} %fusion.25), channel_id=3, replica_groups=mesh['mkt'=32,'draw'=4,'nest'=2] {'nest'}, dimensions={0}, use_global_device_ids=true | all-gather | bytes 49152 | tf_op jit(solution)/shard_map/all_gather | solution.py:26
  114.5 6.9 %bitcast_multiply_fusion.1 = f32[32,384,128]{2,1,0:T(8,128)} fusion(f32[32,8,128]{2,1,0:T(8,128)S(1)} %multiply_divide_fusion.1, f32[384]{0:T(512)S(1)} %reshape.118, f32[32,384,128]{2,1,0:T(8,128)} %get-tuple-element.13, f32[32,384]{1,0:T(8,128)S(1)} %copy.38, f32[384]{0:T(512)S(1)} %convert_element_type.20), kind=kLoop, calls=%fused_computation.2 | loop fusion | flops 6291456 | bytes 12766208 | tf_op jit(solution)/shard_map/mul | solution.py:86
  121.4 4.5 %reduce_sum.153 = f32[32,384]{1,0:T(8,128)S(1)} reduce(f32[32,384,128]{2,1,0:T(8,128)} %bitcast_multiply_fusion.1, f32[]{:T(128)} %constant.18.clone.1), dimensions={2}, to_apply=%region_9.10 | reduce | flops 1560576 | bytes 6340612 | tf_op jit(solution)/shard_map/reduce_sum | solution.py:86
  125.9 8.7 %all_to_all.57 = f32[4,32,384]{2,1,0:T(8,128)S(1)} all-to-all(f32[4,32,384]{2,1,0:T(8,128)S(1)} %broadcast_in_dim.101), channel_id=1, replica_groups=mesh['mkt'=32,'draw'=4,'nest'=2] {'draw'}, dimensions={0} | all-to-all | bytes 393216 | tf_op jit(solution)/shard_map/all_to_all | solution.py:11
  135.1 6.8 %exponential_multiply_fusion = f32[32,384,128]{2,1,0:T(8,128)} fusion(f32[32,384,128]{2,1,0:T(8,128)} %get-tuple-element.13, f32[32,384]{1,0:T(8,128)S(1)} %copy.40, f32[384]{0:T(512)S(1)} %reshape.118, f32[384]{0:T(512)S(1)} %convert_element_type.20), kind=kLoop, calls=%fused_computation.4 | loop fusion | flops 4718592 | bytes 12635136 | tf_op jit(solution)/shard_map/mul | solution.py:78
  141.9 3.7 %reduce_sum.155 = f32[32,8,128]{2,1,0:T(8,128)S(1)} reduce(f32[32,8,48,128]{3,2,1,0:T(8,128)} %bitcast.71, f32[]{:T(128)} %constant.18.clone.1), dimensions={2}, to_apply=%region_11.12 | reduce | flops 1540096 | bytes 6422532 | tf_op jit(solution)/shard_map/reduce_sum | solution.py:82
  145.7 5.9 %all-gather.2 = f32[64,128]{1,0:T(8,128)S(1)} all-gather(f32[32,128]{1,0:T(8,128)S(1)} %fusion.24), channel_id=4, replica_groups=mesh['mkt'=32,'draw'=4,'nest'=2] {'nest'}, dimensions={0}, use_global_device_ids=true | all-gather | bytes 49152 | tf_op jit(solution)/shard_map/all_gather | solution.py:26
  151.7 6.9 %bitcast_multiply_fusion = f32[32,384,128]{2,1,0:T(8,128)} fusion(f32[32,8,128]{2,1,0:T(8,128)S(1)} %multiply_divide_fusion, f32[384]{0:T(512)S(1)} %reshape.118, f32[32,384,128]{2,1,0:T(8,128)} %get-tuple-element.13, f32[32,384]{1,0:T(8,128)S(1)} %copy.40, f32[384]{0:T(512)S(1)} %convert_element_type.20), kind=kLoop, calls=%fused_computation.1 | loop fusion | flops 6291456 | bytes 12766208 | tf_op jit(solution)/shard_map/mul | solution.py:86
  158.7 4.5 %reduce_sum.158 = f32[32,384]{1,0:T(8,128)S(1)} reduce(f32[32,384,128]{2,1,0:T(8,128)} %bitcast_multiply_fusion, f32[]{:T(128)} %constant.18.clone.1), dimensions={2}, to_apply=%region_14.15 | reduce | flops 1560576 | bytes 6340612 | tf_op jit(solution)/shard_map/reduce_sum | solution.py:86
  163.2 8.7 %all_to_all.58 = f32[4,32,384]{2,1,0:T(8,128)S(1)} all-to-all(f32[4,32,384]{2,1,0:T(8,128)S(1)} %broadcast_in_dim.102), channel_id=1, replica_groups=mesh['mkt'=32,'draw'=4,'nest'=2] {'draw'}, dimensions={0} | all-to-all | bytes 393216 | tf_op jit(solution)/shard_map/all_to_all | solution.py:11
  (59 shorter events, 8.6 us)
Async XLA Ops:
  0.6 1.2 copy-start
  0.6 42.1 %copy-start.2 = (s32[8,48]{1,0:T(8,128)S(1)}, s32[8,48]{1,0:T(8,128)}, u32[]{:S(2)}) copy-start(s32[8,48]{1,0:T(8,128)} %param.10) | copy-start | bytes 4612
  0.7 42.1 %copy-start.1 = (f32[8]{0:T(128)S(1)}, f32[8]{0:T(128)}, u32[]{:S(2)}) copy-start(f32[8]{0:T(128)} %param.9) | copy-start | bytes 100
  2.6 57.1 %copy-start.3 = (bf16[32,32,128]{2,1,0:T(8,128)(2,1)S(1)}, bf16[32,32,128]{2,1,0:T(8,128)(2,1)}, u32[]{:S(2)}) copy-start(bf16[32,32,128]{2,1,0:T(8,128)(2,1)} %param.7) | copy-start | bytes 786436
  2.6 57.1 %copy-start.4 = (f32[32]{0:T(128)S(1)}, f32[32]{0:T(128)}, u32[]{:S(2)}) copy-start(f32[32]{0:T(128)} %param.8) | copy-start | bytes 388
  4.4 19.3 %all-to-all-start.1 = ((bf16[32,2,1024]{2,1,0:T(2,128)(2,1)}), bf16[32,2,1024]{2,1,0:T(2,128)(2,1)S(1)}, u32[]{:S(2)}, u32[]{:S(2)}) async-start(bf16[32,2,1024]{2,1,0:T(2,128)(2,1)} %reshape.136), calls=%async_computation.1 | async-start | bytes 262144 | tf_op jit(solution)/shard_map/all_to_all | solution.py:45
  23.7 11.9 %all-to-all-start = ((f32[32,1,512]{2,1,0:T(1,128)}), f32[32,1,512]{2,1,0:T(1,128)S(1)}, u32[]{:S(2)}, u32[]{:S(2)}) async-start(f32[32,1,512]{2,1,0:T(1,128)} %reshape.138), calls=%async_computation | async-start | bytes 131072 | tf_op jit(solution)/shard_map/all_to_all | solution.py:47
  36.7 23.0 %all-to-all-start.2 = ((bf16[8,4,512,32]{2,3,1,0:T(8,128)(2,1)}), bf16[8,4,512,32]{2,3,1,0:T(8,128)(2,1)S(1)}, u32[]{:S(2)}, u32[]{:S(2)}) async-start(bf16[8,4,512,32]{2,3,1,0:T(8,128)(2,1)} %broadcast_in_dim.98), calls=%async_computation.2 | async-start | bytes 2097152 | tf_op jit(solution)/shard_map/all_to_all | solution.py:11
  87.7 9.7 %all-to-all-start.3 = ((f32[4,32,384]{2,1,0:T(8,128)}), f32[4,32,384]{2,1,0:T(8,128)S(1)}, u32[]{:S(2)}, u32[]{:S(2)}) async-start(f32[4,32,384]{2,1,0:T(8,128)} %broadcast_in_dim.99), calls=%async_computation.3 | async-start | bytes 393216 | tf_op jit(solution)/shard_map/all_to_all | solution.py:11
where the time goes:
time: 175 us; the launch traced here: 174 us
  other arithmetic  61.3 us (35%)
  blocking collectives  35.1 us (20%)
  waiting for transfers between devices  32.7 us (19%)
  starting transfers between devices  23.6 us (13%)
  local copies, waits for them, and re-layouts  13.2 us (8%)
  matrix products  6.84 us (4%)
    mul x3, other arithmetic, shards(): grouped * nest_ratio[:, :, None, :]  20.1 us
    all_to_all x2, waiting for transfers between devices, copy_for_each(): return lax.all_to_all(copies, axis, split_axis=0, concat_axis=0, tiled=True)  19.8 us
    all_gather x3, blocking collectives, over_pieces(): pieces = lax.all_gather(value, axis)  17.7 us
    all_to_all x2, blocking collectives, copy_for_each(): return lax.all_to_all(copies, axis, split_axis=0, concat_axis=0, tiled=True)  17.4 us
    mul x2, other arithmetic, shards(): live_flag[None, :, None]  13.6 us
    reduce_sum x3, other arithmetic, shards(): jnp.sum(grouped * nest_ratio[:, :, None, :], axis=3)  13.4 us
    reduce_sum x3, other arithmetic, shards(): inner_sum = jnp.sum(grouped, axis=2)  11 us
    all_to_all x1, starting transfers between devices, shards(): lax.all_to_all(portion, 'mkt', split_axis=2, concat_axis=1, tiled=True)  10.1 us
  transfers between devices with their start and end apart: 4, of which 4 were waited for; matrix products, arithmetic and copies ran while one was open for 4% of the time, Pallas kernels for 0%

commit v1 on v0

v1 whole, which is shorter than its diff:
```python
import functools
import math

import jax
import jax.numpy as jnp
from jax import lax
from jax.experimental import pallas as pl
from jax.experimental.pallas import tpu as pltpu
from jax.sharding import PartitionSpec as P

ITERS = 3
BLOCKS = 32
QUAD = 4
K = 32
PROD = 16
SLOTS = 48
NESTS = 16
HALF = 8
DRAWS = 512
MARKETS = 1024
LANES = 128
ROWS = 24
LOG2E = 1.0 / math.log(2.0)
LOW = -1e30
TINY = 1.1754944e-38
f32, bf16, i32 = jnp.float32, jnp.bfloat16, jnp.int32
VMEM = pl.BlockSpec(memory_space=pltpu.VMEM)
SMEM = pl.BlockSpec(memory_space=pltpu.SMEM)


def iota(shape, dim):
    return lax.broadcasted_iota(i32, shape, dim)


def dot(a, b):
    return lax.dot_general(a, b, (((1,), (0,)), ((), ())), preferred_element_type=f32)


def dot_t(a, b):
    return lax.dot_general(a, b, (((1,), (1,)), ((), ())), preferred_element_type=f32)


def pack(me_ref, f_ref, l_ref, out_ref, g_ref, o_ref, s_ref):
    base = me_ref[0] * QUAD
    market = iota((MARKETS, LANES), 0)
    lane = iota((MARKETS, LANES), 1)
    pick = jnp.where(market == (lane % BLOCKS) * 32 + base + lane // BLOCKS, 1.0, 0.0).astype(bf16)
    g_ref[...] = dot(f_ref[...].reshape(K * PROD, MARKETS), pick)
    log = l_ref[...]
    high = log.astype(bf16)
    rest = log - high.astype(f32)
    middle = rest.astype(bf16)
    low = (rest - middle.astype(f32)).astype(bf16)
    logs = dot(jnp.concatenate([high, middle, low], axis=0), pick)
    spread = jnp.where(iota((BLOCKS, LANES), 0) == iota((BLOCKS, LANES), 1) % BLOCKS, 1.0, 0.0).astype(bf16)
    own = iota((LANES, LANES), 0) // K == iota((LANES, LANES), 1) // BLOCKS
    for j in range(PROD):
        part = g_ref[pl.ds(j, K, stride=PROD), :]
        part = jnp.where(own, jnp.concatenate([part] * QUAD, axis=0), 0.0).astype(bf16)
        o_ref[pl.ds(j, BLOCKS, stride=PROD), :] = dot_t(spread, part)
    out_ref[:, :PROD, :] = o_ref[...].reshape(BLOCKS, PROD, LANES).astype(bf16)
    own = (iota((LANES, LANES), 0) // PROD) % QUAD == iota((LANES, LANES), 1) // BLOCKS
    first = jnp.concatenate([logs[:PROD]] * QUAD + [logs[PROD : 2 * PROD]] * QUAD, axis=0)
    second = jnp.concatenate([logs[2 * PROD :]] * QUAD + [jnp.zeros((64, LANES), f32)], axis=0)
    s_ref[...] = jnp.zeros_like(s_ref)
    s_ref[pl.ds(0, BLOCKS, stride=8), :] = dot_t(spread, jnp.where(own, first, 0.0).astype(bf16))
    s_ref[pl.ds(1, BLOCKS, stride=8), :] = dot_t(spread, jnp.where(own, second, 0.0).astype(bf16))
    out_ref[:, PROD:, :] = s_ref[...].reshape(BLOCKS, 8, LANES).astype(bf16)


def across(x):
    return jnp.concatenate([x] * (DRAWS // LANES), axis=1)


def contract(me_ref, x_ref, t0_ref, t1_ref, t2_ref, t3_ref, scale_ref, near_ref, far_ref, out_ref,
             hot_ref, slot_ref, taste_ref, mu_ref, e_ref, v_ref, t_ref, s_ref, l_ref, y_ref):
    near, far = near_ref[...], far_ref[...]
    first = me_ref[1] == 0
    table = jnp.concatenate([jnp.where(first, near, far), jnp.where(first, far, near)], axis=0)
    rate = jnp.broadcast_to(table[:, SLOTS : SLOTS + 1], (NESTS, LANES))
    to_two = LOG2E / rate
    gain = (1.0 - rate) * to_two
    ids = table.astype(i32)
    wide = iota((NESTS, DRAWS), 1)
    narrow = iota((NESTS, LANES), 1)

    for t in range(SLOTS):
        here = jnp.broadcast_to(ids[:, t : t + 1], (NESTS, LANES))
        hot_ref[t * NESTS : (t + 1) * NESTS, :] = jnp.where(across(here) == wide, 1.0, 0.0).astype(bf16)
    x = x_ref[:, :PROD, :].reshape(BLOCKS * PROD, LANES)
    slot_ref[...] = dot(hot_ref[...], x).astype(bf16)

    l_ref[...] = x_ref[:, PROD:, :].astype(f32).reshape(BLOCKS * 8, LANES)
    top = l_ref[pl.ds(0, BLOCKS, stride=8), :]
    rest = l_ref[pl.ds(1, BLOCKS, stride=8), :]
    both = jnp.concatenate([top, rest], axis=1).astype(bf16)
    for t in range(SLOTS):
        here = jnp.broadcast_to(ids[:, t : t + 1], (NESTS, LANES))
        y_ref[t * NESTS : (t + 1) * NESTS, :] = jnp.where((here >> 4) == narrow, 1.0, 0.0).astype(bf16)
    rows = dot(y_ref[:, :BLOCKS], both)
    lane2 = iota((NESTS, 2 * LANES), 1) % PROD
    for t in range(SLOTS):
        here = jnp.broadcast_to(ids[:, t : t + 1], (NESTS, LANES)) & 15
        here = jnp.concatenate([here, here], axis=1)
        cut = rows[t * NESTS : (t + 1) * NESTS, :]
        slot = jnp.where(here == lane2, cut, 0.0).astype(bf16)
        hot_ref[t * NESTS : (t + 1) * NESTS, : 2 * LANES] = slot
    copies = jnp.where(
        (iota((2 * LANES, DRAWS), 0) // PROD) % QUAD == iota((2 * LANES, DRAWS), 1) // LANES, 1.0, 0.0
    ).astype(bf16)
    target = dot(hot_ref[:, : 2 * LANES], copies)
    whole = (top + pltpu.roll(top, 64, 1)) + rest
    shares = jnp.exp(whole)
    column = iota((BLOCKS, LANES), 1)
    for q in range(QUAD):
        inside = jnp.where(column // PROD == q, shares, 0.0)
        outside = 1.0 - jnp.sum(jnp.sum(inside, axis=1, keepdims=True), axis=0, keepdims=True)
        outside = jnp.broadcast_to(jnp.log(outside), (NESTS, LANES))
        for t in range(SLOTS):
            here = jnp.broadcast_to(ids[:, t : t + 1], (NESTS, LANES))
            goal = target[t * NESTS : (t + 1) * NESTS, q * LANES : (q + 1) * LANES]
            t_ref[q, t] = goal + math.log(DRAWS)
            v_ref[q, t] = jnp.where(here >= 0, (goal - outside) * to_two, LOW)

    square = iota((K, K), 0) == iota((K, K), 1)
    scale = jnp.sum(jnp.where(square, jnp.broadcast_to(scale_ref[...], (K, K)), 0.0), axis=1, keepdims=True)
    scale = jnp.broadcast_to(scale, (K, LANES))
    taste_ref[...] = jnp.zeros_like(taste_ref)
    for q in range(QUAD):
        for b, ref in enumerate((t0_ref, t1_ref, t2_ref, t3_ref)):
            taste = (scale * ref[q].astype(f32)).astype(bf16)
            taste_ref[q, q * K : (q + 1) * K, b * LANES : (b + 1) * LANES] = taste
    for q in range(QUAD):
        mu = dot(slot_ref[...], taste_ref[q])
        mu_ref[q] = mu.reshape(SLOTS, NESTS, DRAWS) * across(to_two)[None]

    less = across(rate - 1.0)

    def step(_, carry):
        for q in range(QUAD):
            inner = jnp.zeros((NESTS, DRAWS), f32)
            for t in range(SLOTS):
                e = jnp.exp2(mu_ref[q, t] + across(v_ref[q, t]))
                e_ref[q, t] = e
                inner = inner + e
            power = jnp.exp2(less * (jnp.log(inner) * LOG2E))
            total = 1.0 + jnp.sum(power * inner, axis=0, keepdims=True)
            weight = power / total
            for t in range(SLOTS):
                p = e_ref[q, t] * weight
                p = (p[:, :128] + p[:, 128:256]) + (p[:, 256:384] + p[:, 384:])
                share = jnp.broadcast_to(jnp.sum(p, axis=1, keepdims=True), (NESTS, LANES))
                s_ref[q, t] = share
                v_ref[q, t] = v_ref[q, t] + gain * (t_ref[q, t] - jnp.log(jnp.maximum(share, TINY)))
        return carry

    lax.fori_loop(0, ITERS, step, 0)
    back = rate * math.log(2.0)
    for q in range(QUAD):
        values = jnp.zeros((NESTS, LANES), f32)
        shares = jnp.zeros((NESTS, LANES), f32)
        for t in range(SLOTS):
            values = jnp.where(narrow == t, v_ref[q, t], values)
            shares = jnp.where(narrow == t + 64, s_ref[q, t], shares)
        values = jnp.where(ids >= 0, values * back, 0.0)
        both = jnp.where(narrow < SLOTS, values, shares * (1.0 / DRAWS))
        for d in range(4):
            for n in range(2):
                out_ref[2 * d + n, q * HALF : (q + 1) * HALF, :] = both[n * HALF : (n + 1) * HALF]


def unpack(r_ref, value_ref, share_ref):
    for g in range(HALF):
        part = r_ref[pl.ds(g, 32, stride=HALF), :]
        value_ref[:, g * SLOTS : (g + 1) * SLOTS] = part[:, :SLOTS]
        share_ref[:, g * SLOTS : (g + 1) * SLOTS] = part[:, 64 : 64 + SLOTS]


def shards(features, taste_draws, taste_scale, nest_param, members, log_share):
    d, n = lax.axis_index("draw"), lax.axis_index("nest")
    me = jnp.stack([d * 2 + n, n]).astype(i32)
    send = pl.pallas_call(
        pack,
        name="pack",
        out_shape=jax.ShapeDtypeStruct((BLOCKS, ROWS, LANES), bf16),
        in_specs=[SMEM, VMEM, VMEM],
        out_specs=VMEM,
        scratch_shapes=[
            pltpu.VMEM((K * PROD, LANES), f32),
            pltpu.VMEM((BLOCKS * PROD, LANES), f32),
            pltpu.VMEM((BLOCKS * 8, LANES), f32),
        ],
    )(me, features, log_share)
    recv = lax.all_to_all(send, "mkt", split_axis=0, concat_axis=0, tiled=True)

    near = jnp.concatenate(
        [members.astype(f32), nest_param[:, None], jnp.zeros((HALF, LANES - SLOTS - 1), f32)], axis=1
    )
    far = lax.ppermute(near, "nest", [(0, 1), (1, 0)])
    tastes = []
    for shift in range(4):
        to = (d + shift) % 4
        piece = lax.dynamic_slice_in_dim(taste_draws, to * 8 + n * QUAD, QUAD, 0)
        if shift:
            piece = lax.ppermute(piece, "draw", [(i, (i + shift) % 4) for i in range(4)])
        tastes.append(piece)

    big = (QUAD, SLOTS, NESTS, DRAWS)
    small = (QUAD, SLOTS, NESTS, LANES)
    results = pl.pallas_call(
        contract,
        name="contract",
        out_shape=jax.ShapeDtypeStruct((8, 32, LANES), f32),
        in_specs=[SMEM] + [VMEM] * 8,
        out_specs=VMEM,
        scratch_shapes=[
            pltpu.VMEM((SLOTS * NESTS, DRAWS), bf16),
            pltpu.VMEM((SLOTS * NESTS, LANES), bf16),
            pltpu.VMEM((QUAD, QUAD * K, DRAWS), bf16),
            pltpu.VMEM(big, f32),
            pltpu.VMEM(big, f32),
            pltpu.VMEM(small, f32),
            pltpu.VMEM(small, f32),
            pltpu.VMEM(small, f32),
            pltpu.VMEM((BLOCKS * 8, LANES), f32),
            pltpu.VMEM((SLOTS * NESTS, LANES), bf16),
        ],
        compiler_params=pltpu.CompilerParams(vmem_limit_bytes=48 * 1024 * 1024),
    )(me, recv, *tastes, taste_scale.reshape(1, K), near, far)
    gathered = lax.all_to_all(results, ("draw", "nest"), split_axis=0, concat_axis=0, tiled=True)
    shape = jax.ShapeDtypeStruct((32, HALF * SLOTS), f32)
    return pl.pallas_call(
        unpack, name="unpack", out_shape=(shape, shape), in_specs=[VMEM], out_specs=(VMEM, VMEM)
    )(gathered.reshape(256, LANES))


def solution(mesh):
    in_specs = (
        P(None, "mkt", None),
        P("mkt", None, "draw"),
        P(),
        P("nest"),
        P("nest", None),
        P("mkt", None),
    )
    out_specs = (P("mkt", "nest"), P("mkt", "nest"))
    return jax.shard_map(shards, mesh=mesh, in_specs=in_specs, out_specs=out_specs, check_vma=False)
```

time: 175 us -> 49.8 us (0.28)
  other arithmetic: 61.3 us -> 0.73 us
  waiting for transfers between devices: 32.7 us -> 3 us
  blocking collectives: 35.1 us -> 13.4 us
  Pallas kernels: 0 us -> 12.5 us
  local copies, waits for them, and re-layouts: 13.2 us -> 0.85 us
  matrix products: 6.84 us -> 0 us
  starting transfers between devices: 23.6 us -> 18.3 us
    mul x5 -> x0, other arithmetic: 33.7 us -> none  [the longest x3 20.1 us: shards(): grouped * nest_ratio[:, :, None, :]]
    all_to_all x4 -> x1, waiting for transfers between devices: 32.7 us -> 0.01 us  [shards(): recv = lax.all_to_all(send, 'mkt', split_axis=0, concat_axis=0, tiled=True)]
    reduce_sum x16 -> x0, other arithmetic: 24.9 us -> none  [the longest x3 13.4 us: shards(): jnp.sum(grouped * nest_ratio[:, :, None, :], axis=3)]
    all_gather x3 -> x0, blocking collectives: 17.7 us -> none  [over_pieces(): pieces = lax.all_gather(value, axis)]
    all_to_all x4 -> x1, starting transfers between devices: 23.6 us -> 10.2 us  [shards(): recv = lax.all_to_all(send, 'mkt', split_axis=0, concat_axis=0, tiled=True)]
    pallas_call x0 -> x3, Pallas kernels: none -> 12.5 us  [the longest x1 7.59 us: shards(): pl.pallas_call(contract, name='contract', out_shape=jax.ShapeDtypeStruct(...]
    ppermute x0 -> x4, starting transfers between devices: none -> 8.04 us  [the longest x3 5.9 us: shards(): lax.ppermute(piece, 'draw', [(i, (i + shift) % 4) for i in range(4)])]
    dot_general x1 -> x0, matrix products: 6.84 us -> none  [shards(): jnp.einsum('dve,dvb->deb', slot_features, taste_matrix, preferred_element...]
  transfers between devices with their start and end apart: 4 -> 5, of which waited for: 4 -> 1; matrix products, arithmetic and copies ran while one was open for 4% -> 1% of each run, Pallas kernels for 0% -> 0%
where the time goes in v1:
time: 49.8 us; the launch traced here: 49.5 us
  starting transfers between devices  18.3 us (37%)
  blocking collectives  13.4 us (27%)
  Pallas kernels  12.5 us (25%)
  waiting for transfers between devices  3 us (6%)
  local copies, waits for them, and re-layouts  0.85 us (2%)
  between operations  0.77 us (2%)
  other arithmetic  0.73 us (1%)
    all_to_all x1, blocking collectives, shards(): lax.all_to_all(results, ('draw', 'nest'), split_axis=0, concat_axis=0, ti...  13.4 us
    all_to_all x1, starting transfers between devices, shards(): recv = lax.all_to_all(send, 'mkt', split_axis=0, concat_axis=0, tiled=True)  10.2 us
    pallas_call x1, Pallas kernels, shards(): pl.pallas_call(contract, name='contract', out_shape=jax.ShapeDtypeStruct(...  7.59 us
    ppermute x3, starting transfers between devices, shards(): lax.ppermute(piece, 'draw', [(i, (i + shift) % 4) for i in range(4)])  5.9 us
    pallas_call x1, Pallas kernels, shards(): pl.pallas_call(pack, name='pack', out_shape=jax.ShapeDtypeStruct((BLOCKS,...  3.27 us
    ppermute x1, waiting for transfers between devices, shards(): far = lax.ppermute(near, 'nest', [(0, 1), (1, 0)])  2.99 us
    ppermute x1, starting transfers between devices, shards(): far = lax.ppermute(near, 'nest', [(0, 1), (1, 0)])  2.14 us
    pallas_call x1, Pallas kernels, shards(): pl.pallas_call(unpack, name='unpack', out_shape=(shape, shape), in_specs=...  1.66 us
  transfers between devices with their start and end apart: 5, of which 1 were waited for; matrix products, arithmetic and copies ran while one was open for 1% of the time, Pallas kernels for 0%

profile of v1, /device:TPU:2, one launch (start us, length us, event | category | flops | bytes accessed | tf_op | source)
XLA Modules:
  0.0 49.5 jit_solution(723198339186633857)
XLA Ops:
  0.6 0.6 %pad_add_fusion.me_ref = s32[2]{0:T(128)} fusion(s32[1]{0:T(128)} %bitcast.1, s32[1]{0:T(128)} %bitcast), kind=kLoop, calls=%fused_computation.5 | loop fusion | flops 2 | bytes 16 | tf_op jit(solution)/shard_map/stack | solution.py:181
  1.3 3.3 %pack.1 = bf16[32,24,128]{2,1,0:T(8,128)(2,1)} custom-call(s32[2]{0:T(128)} %pad_add_fusion.me_ref, bf16[32,16,1024]{2,1,0:T(8,128)(2,1)} %f_ref.1, f32[16,1024]{1,0:T(8,128)} %l_ref.1), custom_call_target="tpu_custom_call" | custom-call | tf_op jit(solution)/shard_map/pack/pallas_call | solution.py:182
  4.6 0.0 copy-start.2
  4.6 10.2 %all-to-all-start = ((bf16[32,24,128]{2,1,0:T(8,128)(2,1)}), bf16[32,24,128]{2,1,0:T(8,128)(2,1)S(1)}, u32[]{:S(2)}, u32[]{:S(2)}) async-start(bf16[32,24,128]{2,1,0:T(8,128)(2,1)} %pack.1), calls=%async_computation | async-start | bytes 393216 | tf_op jit(solution)/shard_map/all_to_all | solution.py:194
  14.8 0.0 copy-done.2
  14.9 0.0 copy-start.4
  14.9 1.7 %collective-permute-start = (bf16[4,32,128]{2,1,0:T(8,128)(2,1)S(1)}, bf16[4,32,128]{2,1,0:T(8,128)(2,1)S(1)}, u32[]{:S(2)}, u32[]{:S(2)}) collective-permute-start(bf16[4,32,128]{2,1,0:T(8,128)(2,1)S(1)} %get-tuple-element.3), channel_id=1, source_target_pairs={{0,2},{2,4},{4,6},{6,0},{1,3},{3,5},{5,7},{7,1},{8,10},{10,12},{12... | collective-permute-start | bytes 98312 | tf_op jit(solution)/shard_map/ppermute | solution.py:205
  16.5 0.0 copy-start.3
  16.6 2.9 %collective-permute-start.1 = (bf16[4,32,128]{2,1,0:T(8,128)(2,1)S(1)}, bf16[4,32,128]{2,1,0:T(8,128)(2,1)S(1)}, u32[]{:S(2)}, u32[]{:S(2)}) collective-permute-start(bf16[4,32,128]{2,1,0:T(8,128)(2,1)S(1)} %get-tuple-element.5), channel_id=1, source_target_pairs={{0,4},{2,6},{4,0},{6,2},{1,5},{3,7},{5,1},{7,3},{8,12},{10,14},{12... | collective-permute-start | bytes 98312 | tf_op jit(solution)/shard_map/ppermute | solution.py:205
  19.5 1.3 %collective-permute-start.2 = (bf16[4,32,128]{2,1,0:T(8,128)(2,1)S(1)}, bf16[4,32,128]{2,1,0:T(8,128)(2,1)S(1)}, u32[]{:S(2)}, u32[]{:S(2)}) collective-permute-start(bf16[4,32,128]{2,1,0:T(8,128)(2,1)S(1)} %get-tuple-element.2), channel_id=1, source_target_pairs={{0,6},{2,0},{4,2},{6,4},{1,7},{3,1},{5,3},{7,5},{8,14},{10,8},{12,... | collective-permute-start | bytes 98312 | tf_op jit(solution)/shard_map/ppermute | solution.py:205
  20.8 0.0 copy-done.4
  20.8 0.1 copy.8
  20.9 0.0 copy-done.3
  20.9 0.1 pad.2.clone
  21.0 0.1 maximum_maximum_fusion.near_ref
  21.0 2.1 %collective-permute-start.3 = (f32[8,128]{1,0:T(8,128)S(1)}, f32[8,128]{1,0:T(8,128)S(1)}, u32[]{:S(2)}, u32[]{:S(2)}) collective-permute-start(f32[8,128]{1,0:T(8,128)S(1)} %maximum_maximum_fusion.near_ref), channel_id=1, source_target_pairs={{0,1},{1,0},{2,3},{3,2},{4,5},{5,4},{6,7},{7,6},{8,9},{9,8},{10,11... | collective-permute-start | bytes 12296 | tf_op jit(solution)/shard_map/ppermute | solution.py:199
  23.2 3.0 %collective-permute-done.3.far_ref = f32[8,128]{1,0:T(8,128)S(1)} collective-permute-done((f32[8,128]{1,0:T(8,128)S(1)}, f32[8,128]{1,0:T(8,128)S(1)}, u32[]{:S(2)}, u32[]{:S(2)}) %collective-permute-start.3) | collective-permute-done | bytes 4128 | tf_op jit(solution)/shard_map/ppermute | solution.py:199
  26.2 0.0 collective-permute-done.t1_ref
  26.2 0.0 collective-permute-done.1.t2_ref
  26.2 0.0 collective-permute-done.2.t3_ref
  26.2 0.0 all-to-all-done.x_ref
  26.2 0.0 copy-start
  26.2 0.0 copy-start.1
  26.2 0.6 %copy-done = s32[2]{0:T(128)S(1)} copy-done((s32[2]{0:T(128)S(1)}, s32[2]{0:T(128)}, u32[]{:S(2)}) %copy-start) | copy-done | bytes 32
  26.9 0.0 copy-done.1
  26.9 7.6 %contract.1 = f32[8,32,128]{2,1,0:T(8,128)S(1)} custom-call(s32[2]{0:T(128)S(1)} %copy-done, bf16[32,24,128]{2,1,0:T(8,128)(2,1)S(1)} %all-to-all-done.x_ref, bf16[4,32,128]{2,1,0:T(8,128)(2,1)S(1)} %get-tuple-element.4.t0_ref, bf16[4,32,128]{2,1,0:T(8,128)(2,1)S(1)} %collective-permute-done.t1_ref, bf16[4,32,128]{2,1,0:T(8,128)(2,1)S(1)} %collective-permute-done.1.t2_ref, ...), custom_call_target="tpu_custom_call" | custom-call | tf_op jit(solution)/shard_map/contract/pallas_call | solution.py:210
  34.5 13.4 %all_to_all.10 = f32[8,32,128]{2,1,0:T(8,128)} all-to-all(f32[8,32,128]{2,1,0:T(8,128)S(1)} %contract.1), channel_id=1, replica_groups=mesh['mkt'=32,'draw'=4,'nest'=2] {'draw','nest'}, dimensions={0} | all-to-all | bytes 262144 | tf_op jit(solution)/shard_map/all_to_all | solution.py:230
  47.8 1.7 %unpack.1 = (f32[32,384]{1,0:T(8,128)}, f32[32,384]{1,0:T(8,128)}) custom-call(f32[256,128]{1,0:T(8,128)} %bitcast.6), custom_call_target="tpu_custom_call" | custom-call | tf_op jit(solution)/shard_map/unpack/pallas_call | solution.py:232
  (3 shorter events, 0.0 us)
Async XLA Ops:
  4.6 10.3 %copy-start.2 = (bf16[32,32,128]{2,1,0:T(8,128)(2,1)S(1)}, bf16[32,32,128]{2,1,0:T(8,128)(2,1)}, u32[]{:S(2)}) copy-start(bf16[32,32,128]{2,1,0:T(8,128)(2,1)} %param.7) | copy-start | bytes 786436
  4.6 21.6 %all-to-all-start = ((bf16[32,24,128]{2,1,0:T(8,128)(2,1)}), bf16[32,24,128]{2,1,0:T(8,128)(2,1)S(1)}, u32[]{:S(2)}, u32[]{:S(2)}) async-start(bf16[32,24,128]{2,1,0:T(8,128)(2,1)} %pack.1), calls=%async_computation | async-start | bytes 393216 | tf_op jit(solution)/shard_map/all_to_all | solution.py:194
  14.9 5.9 %copy-start.4 = (f32[8]{0:T(128)S(1)}, f32[8]{0:T(128)}, u32[]{:S(2)}) copy-start(f32[8]{0:T(128)} %param.9) | copy-start | bytes 100
  14.9 11.3 %collective-permute-start = (bf16[4,32,128]{2,1,0:T(8,128)(2,1)S(1)}, bf16[4,32,128]{2,1,0:T(8,128)(2,1)S(1)}, u32[]{:S(2)}, u32[]{:S(2)}) collective-permute-start(bf16[4,32,128]{2,1,0:T(8,128)(2,1)S(1)} %get-tuple-element.3), channel_id=1, source_target_pairs={{0,2},{2,4},{4,6},{6,0},{1,3},{3,5},{5,7},{7,1},{8,10},{10,12},{12... | collective-permute-start | bytes 98312 | tf_op jit(solution)/shard_map/ppermute | solution.py:205
  16.5 4.3 %copy-start.3 = (s32[8,48]{1,0:T(8,128)S(1)}, s32[8,48]{1,0:T(8,128)}, u32[]{:S(2)}) copy-start(s32[8,48]{1,0:T(8,128)} %param.10) | copy-start | bytes 4612
  16.6 9.6 %collective-permute-start.1 = (bf16[4,32,128]{2,1,0:T(8,128)(2,1)S(1)}, bf16[4,32,128]{2,1,0:T(8,128)(2,1)S(1)}, u32[]{:S(2)}, u32[]{:S(2)}) collective-permute-start(bf16[4,32,128]{2,1,0:T(8,128)(2,1)S(1)} %get-tuple-element.5), channel_id=1, source_target_pairs={{0,4},{2,6},{4,0},{6,2},{1,5},{3,7},{5,1},{7,3},{8,12},{10,14},{12... | collective-permute-start | bytes 98312 | tf_op jit(solution)/shard_map/ppermute | solution.py:205
  19.5 6.7 %collective-permute-start.2 = (bf16[4,32,128]{2,1,0:T(8,128)(2,1)S(1)}, bf16[4,32,128]{2,1,0:T(8,128)(2,1)S(1)}, u32[]{:S(2)}, u32[]{:S(2)}) collective-permute-start(bf16[4,32,128]{2,1,0:T(8,128)(2,1)S(1)} %get-tuple-element.2), channel_id=1, source_target_pairs={{0,6},{2,0},{4,2},{6,4},{1,7},{3,1},{5,3},{7,5},{8,14},{10,8},{12,... | collective-permute-start | bytes 98312 | tf_op jit(solution)/shard_map/ppermute | solution.py:205
  21.0 5.1 %collective-permute-start.3 = (f32[8,128]{1,0:T(8,128)S(1)}, f32[8,128]{1,0:T(8,128)S(1)}, u32[]{:S(2)}, u32[]{:S(2)}) collective-permute-start(f32[8,128]{1,0:T(8,128)S(1)} %maximum_maximum_fusion.near_ref), channel_id=1, source_target_pairs={{0,1},{1,0},{2,3},{3,2},{4,5},{5,4},{6,7},{7,6},{8,9},{9,8},{10,11... | collective-permute-start | bytes 12296 | tf_op jit(solution)/shard_map/ppermute | solution.py:199
  26.2 0.7 %copy-start = (s32[2]{0:T(128)S(1)}, s32[2]{0:T(128)}, u32[]{:S(2)}) copy-start(s32[2]{0:T(128)} %pad_add_fusion.me_ref) | copy-start | bytes 28
  26.2 0.7 %copy-start.1 = (f32[32]{0:T(128)S(1)}, f32[32]{0:T(128)}, u32[]{:S(2)}) copy-start(f32[32]{0:T(128)} %param.8) | copy-start | bytes 388

commit v2 on v1

v2 whole, which is shorter than its diff:
```python
import functools
import math

import jax
import jax.numpy as jnp
from jax import lax
from jax.experimental import pallas as pl
from jax.experimental.pallas import tpu as pltpu
from jax.sharding import PartitionSpec as P

ITERS = 3
BLOCKS = 32
QUAD = 4
K = 32
PROD = 16
SLOTS = 48
NESTS = 16
HALF = 8
DRAWS = 512
MARKETS = 1024
LANES = 128
ROWS = 24
LOG2E = 1.0 / math.log(2.0)
LOW = -1e30
TINY = 1.1754944e-38
EMPTY = 32 * 16 + 15
PLACES = [(o, t) for o in range(2) for t in range(SLOTS)]
f32, bf16, i32 = jnp.float32, jnp.bfloat16, jnp.int32
VMEM = pl.BlockSpec(memory_space=pltpu.VMEM)


def iota(shape, dim):
    return lax.broadcasted_iota(i32, shape, dim)


def dot(a, b):
    return lax.dot_general(a, b, (((1,), (0,)), ((), ())), preferred_element_type=f32)


def dot_t(a, b):
    return lax.dot_general(a, b, (((1,), (1,)), ((), ())), preferred_element_type=f32)


def pack(f_ref, l_ref, out_ref, g_ref, o_ref, s_ref):
    base = (lax.axis_index("draw") * 2 + lax.axis_index("nest")) * QUAD
    market = iota((MARKETS, LANES), 0)
    lane = iota((MARKETS, LANES), 1)
    pick = jnp.where(market == (lane % BLOCKS) * 32 + base + lane // BLOCKS, 1.0, 0.0).astype(bf16)
    g_ref[...] = dot(f_ref[...].reshape(K * PROD, MARKETS), pick)
    log = l_ref[...]
    high = log.astype(bf16)
    rest = log - high.astype(f32)
    middle = rest.astype(bf16)
    low = (rest - middle.astype(f32)).astype(bf16)
    logs = dot(jnp.concatenate([high, middle, low], axis=0), pick)
    spread = jnp.where(iota((BLOCKS, LANES), 0) == iota((BLOCKS, LANES), 1) % BLOCKS, 1.0, 0.0).astype(bf16)
    own = iota((LANES, LANES), 0) // K == iota((LANES, LANES), 1) // BLOCKS
    for j in range(PROD):
        part = g_ref[pl.ds(j, K, stride=PROD), :]
        part = jnp.where(own, jnp.concatenate([part] * QUAD, axis=0), 0.0).astype(bf16)
        o_ref[pl.ds(j, BLOCKS, stride=PROD), :] = dot_t(spread, part)
    out_ref[:, :PROD, :] = o_ref[...].reshape(BLOCKS, PROD, LANES).astype(bf16)
    own = (iota((LANES, LANES), 0) // PROD) % QUAD == iota((LANES, LANES), 1) // BLOCKS
    first = jnp.concatenate([logs[:PROD]] * QUAD + [logs[PROD : 2 * PROD]] * QUAD, axis=0)
    second = jnp.concatenate([logs[2 * PROD :]] * QUAD + [jnp.zeros((64, LANES), f32)], axis=0)
    s_ref[...] = jnp.zeros_like(s_ref)
    s_ref[pl.ds(0, BLOCKS, stride=8), :] = dot_t(spread, jnp.where(own, first, 0.0).astype(bf16))
    s_ref[pl.ds(1, BLOCKS, stride=8), :] = dot_t(spread, jnp.where(own, second, 0.0).astype(bf16))
    out_ref[:, PROD:, :] = s_ref[...].reshape(BLOCKS, 8, LANES).astype(bf16)


def across(x):
    return jnp.concatenate([x] * (DRAWS // LANES), axis=1)


def arrange(near_ref, far_ref, scale_ref, table_ref, hot_ref, pick_ref, mask_ref):
    near, far = near_ref[...], far_ref[...]
    first = lax.axis_index("nest") == 0
    table = jnp.concatenate([jnp.where(first, near, far), jnp.where(first, far, near)], axis=0)
    table_ref[:NESTS, :] = table
    square = iota((K, K), 0) == iota((K, K), 1)
    scale = jnp.sum(jnp.where(square, jnp.broadcast_to(scale_ref[...], (K, K)), 0.0), axis=1, keepdims=True)
    table_ref[NESTS:, :] = jnp.broadcast_to(scale, (K, LANES))
    ids = table.astype(i32)
    ids = jnp.where(ids < 0, EMPTY, ids)
    wide, narrow = iota((HALF, DRAWS), 1), iota((HALF, LANES), 1)
    for b in range(0, len(PLACES), 2):
        hot, pick, mask = [], [], []
        for o, t in PLACES[b : b + 2]:
            here = jnp.broadcast_to(ids[o * HALF : (o + 1) * HALF, t : t + 1], (HALF, LANES))
            hot.append(jnp.where(across(here) == wide, 1.0, 0.0))
            pick.append(jnp.where((here >> 4) == narrow, 1.0, 0.0))
            mask.append(jnp.where((here & 15) == (narrow & 15), 1.0, 0.0))
        rows = slice(b * HALF, (b + 2) * HALF)
        hot_ref[rows, :] = jnp.concatenate(hot, axis=0).astype(bf16)
        pick_ref[rows, :] = jnp.concatenate(pick, axis=0).astype(bf16)
        mask_ref[rows, :] = jnp.concatenate(mask, axis=0).astype(bf16)


def contract(x_ref, t0_ref, t1_ref, t2_ref, t3_ref, table_ref, hot_ref, pick_ref, mask_ref, out_ref,
             slot_ref, taste_ref, mu_ref, e_ref, v_ref, t_ref, l_ref):
    table = [table_ref[o * HALF : (o + 1) * HALF, :] for o in range(2)]
    rate = [jnp.broadcast_to(x[:, SLOTS : SLOTS + 1], (HALF, LANES)) for x in table]
    inverse = [1.0 / x for x in rate]
    to_two = [across(LOG2E * x) for x in inverse]
    gain = [(1.0 - x) * y for x, y in zip(rate, inverse)]
    less = [across(x - 1.0) for x in rate]
    narrow = iota((HALF, LANES), 1)

    l_ref[...] = x_ref[:, PROD:, :].astype(f32).reshape(BLOCKS * 8, LANES)
    top = l_ref[pl.ds(0, BLOCKS, stride=8), :]
    rest = l_ref[pl.ds(1, BLOCKS, stride=8), :]
    both = jnp.concatenate([top, rest], axis=1)
    lane = iota((BLOCKS, 2 * LANES), 1)
    lows = (iota((BLOCKS, 2 * LANES), 0) == 0) & (lane < 64) & (lane % PROD == PROD - 1)
    both = jnp.concatenate([both, jnp.where(lows, LOW, 0.0), jnp.zeros((64, 2 * LANES), f32)], axis=0).astype(bf16)
    rows = dot(pick_ref[...], both).astype(bf16)
    mask = mask_ref[...]
    rows = rows * jnp.concatenate([mask, mask], axis=1)
    copies = jnp.where(
        (iota((2 * LANES, DRAWS), 0) // PROD) % QUAD == iota((2 * LANES, DRAWS), 1) // LANES, 1.0, 0.0
    ).astype(bf16)
    target = dot(rows, copies)
    whole = (top + pltpu.roll(top, 64, 1)) + rest
    shares = jnp.exp(whole)
    column = iota((BLOCKS, LANES), 1)
    outside = []
    for q in range(QUAD):
        inside = jnp.where(column // PROD == q, shares, 0.0)
        total = 1.0 - jnp.sum(jnp.sum(inside, axis=1, keepdims=True), axis=0, keepdims=True)
        outside.append(lax.log2(jnp.broadcast_to(total, (HALF, LANES))))

    x = x_ref[:, :PROD, :].reshape(BLOCKS * PROD, LANES)
    slot_ref[...] = dot(hot_ref[...], x).astype(bf16)
    scale = table_ref[NESTS:, :]
    taste_ref[...] = jnp.zeros_like(taste_ref)
    for q in range(QUAD):
        for b, ref in enumerate((t0_ref, t1_ref, t2_ref, t3_ref)):
            taste = (scale * ref[q].astype(f32)).astype(bf16)
            taste_ref[q, q * K : (q + 1) * K, b * LANES : (b + 1) * LANES] = taste

    def weights(inner):
        power = [jnp.exp2(x * lax.log2(y)) for x, y in zip(less, inner)]
        total = jnp.sum(power[0] * inner[0] + power[1] * inner[1], axis=0, keepdims=True)
        total = (1.0 + total) * DRAWS
        return [x / total for x in power]

    def first_half(q, b, inner, value, mu):
        o = PLACES[b][0]
        e = jnp.exp2(mu + across(value))
        e_ref[q, b] = e
        inner[o] = inner[o] + e

    def second_half(q, b, weight):
        o = PLACES[b][0]
        p = e_ref[q, b] * weight[o]
        p = (p[:, :128] + p[:, 128:256]) + (p[:, 256:384] + p[:, 384:])
        share = jnp.broadcast_to(jnp.sum(p, axis=1, keepdims=True), (HALF, LANES))
        value = v_ref[q, b] + gain[o] * (t_ref[q, b] - lax.log2(jnp.maximum(share, TINY)))
        return value, share

    zeros = jnp.zeros((HALF, DRAWS), f32)
    weight = [None] * QUAD
    count = len(PLACES)
    for q in range(QUAD):
        mu = dot(slot_ref[...], taste_ref[q])
        inner = [zeros, zeros]
        for b, (o, _) in enumerate(PLACES):
            part = mu[b * HALF : (b + 1) * HALF] * to_two[o]
            mu_ref[q, b] = part
            goal = target[b * HALF : (b + 1) * HALF, q * LANES : (q + 1) * LANES] * LOG2E
            t_ref[q, b] = goal
            value = (goal - outside[q]) * inverse[o]
            v_ref[q, b] = value
            first_half(q, b, inner, value, part)
        weight[q] = weights(inner)

    for _ in range(ITERS - 1):
        old = list(weight)
        for q in range(QUAD + 1):
            inner = [zeros, zeros]
            for b in range(count):
                if q < QUAD:
                    v_ref[q, b] = second_half(q, b, old[q])[0]
                if q:
                    first_half(q - 1, b, inner, v_ref[q - 1, b], mu_ref[q - 1, b])
            if q:
                weight[q - 1] = weights(inner)

    back = [x * math.log(2.0) for x in rate]
    for q in range(QUAD):
        values = [jnp.zeros((HALF, LANES), f32)] * 2
        shares = [jnp.zeros((HALF, LANES), f32)] * 2
        for b, (o, t) in enumerate(PLACES):
            value, share = second_half(q, b, weight[q])
            values[o] = jnp.where(narrow == t, value, values[o])
            shares[o] = jnp.where(narrow == t + 64, share, shares[o])
        for n in range(2):
            value = jnp.where(table[n] >= 0.0, values[n] * back[n], 0.0)
            both = jnp.where(narrow < SLOTS, value, shares[n])
            for d in range(4):
                out_ref[2 * d + n, q * HALF : (q + 1) * HALF, :] = both


def unpack(r_ref, value_ref, share_ref):
    for g in range(HALF):
        part = r_ref[pl.ds(g, 32, stride=HALF), :]
        value_ref[:, g * SLOTS : (g + 1) * SLOTS] = part[:, :SLOTS]
        share_ref[:, g * SLOTS : (g + 1) * SLOTS] = part[:, 64 : 64 + SLOTS]


def shards(features, taste_draws, taste_scale, nest_param, members, log_share):
    send = pl.pallas_call(
        pack,
        name="pack",
        out_shape=jax.ShapeDtypeStruct((BLOCKS, ROWS, LANES), bf16),
        in_specs=[VMEM, VMEM],
        out_specs=VMEM,
        scratch_shapes=[
            pltpu.VMEM((K * PROD, LANES), f32),
            pltpu.VMEM((BLOCKS * PROD, LANES), f32),
            pltpu.VMEM((BLOCKS * 8, LANES), f32),
        ],
    )(features, log_share)
    recv = lax.all_to_all(send, "mkt", split_axis=0, concat_axis=0, tiled=True)

    near = jnp.concatenate(
        [members.astype(f32), nest_param[:, None], jnp.zeros((HALF, LANES - SLOTS - 1), f32)], axis=1
    )
    far = lax.ppermute(near, "nest", [(0, 1), (1, 0)])
    rows = len(PLACES) * HALF
    plan = pl.pallas_call(
        arrange,
        name="arrange",
        out_shape=(
            jax.ShapeDtypeStruct((NESTS + K, LANES), f32),
            jax.ShapeDtypeStruct((rows, DRAWS), bf16),
            jax.ShapeDtypeStruct((rows, LANES), bf16),
            jax.ShapeDtypeStruct((rows, LANES), bf16),
        ),
        in_specs=[VMEM] * 3,
        out_specs=(VMEM,) * 4,
        cost_estimate=pl.CostEstimate(flops=2_000_000, bytes_accessed=2_000_000, transcendentals=0),
    )(near, far, taste_scale.reshape(1, K))
    d, n = lax.axis_index("draw"), lax.axis_index("nest")
    tastes = []
    for shift in range(4):
        to = (d + shift) % 4
        piece = lax.dynamic_slice_in_dim(taste_draws, to * 8 + n * QUAD, QUAD, 0)
        if shift:
            piece = lax.ppermute(piece, "draw", [(i, (i + shift) % 4) for i in range(4)])
        tastes.append(piece)

    big = (QUAD, len(PLACES), HALF, DRAWS)
    small = (QUAD, len(PLACES), HALF, LANES)
    results = pl.pallas_call(
        contract,
        name="contract",
        out_shape=jax.ShapeDtypeStruct((8, 32, LANES), f32),
        in_specs=[VMEM] * 9,
        out_specs=VMEM,
        scratch_shapes=[
            pltpu.VMEM((rows, LANES), bf16),
            pltpu.VMEM((QUAD, QUAD * K, DRAWS), bf16),
            pltpu.VMEM(big, f32),
            pltpu.VMEM(big, f32),
            pltpu.VMEM(small, f32),
            pltpu.VMEM(small, f32),
            pltpu.VMEM((BLOCKS * 8, LANES), f32),
        ],
        compiler_params=pltpu.CompilerParams(vmem_limit_bytes=40 * 1024 * 1024),
    )(recv, *tastes, *plan)
    gathered = lax.all_to_all(results, ("draw", "nest"), split_axis=0, concat_axis=0, tiled=True)
    shape = jax.ShapeDtypeStruct((32, HALF * SLOTS), f32)
    return pl.pallas_call(
        unpack, name="unpack", out_shape=(shape, shape), in_specs=[VMEM], out_specs=(VMEM, VMEM)
    )(gathered.reshape(256, LANES))


def solution(mesh):
    in_specs = (
        P(None, "mkt", None),
        P("mkt", None, "draw"),
        P(),
        P("nest"),
        P("nest", None),
        P("mkt", None),
    )
    out_specs = (P("mkt", "nest"), P("mkt", "nest"))
    return jax.shard_map(shards, mesh=mesh, in_specs=in_specs, out_specs=out_specs, check_vma=False)
```

time: 49.8 us -> 52.2 us (1.048)
  local copies, waits for them, and re-layouts: 0.85 us -> 4.5 us
  other arithmetic: 0.73 us -> 0.08 us
  starting transfers between devices: 18.3 us -> 17.7 us
  blocking collectives: 13.4 us -> 12.8 us
    unnamed x10 -> x18, local copies, waits for them, and re-layouts: 0.67 us -> 4.32 us
    pallas_call x0 -> x1, Pallas kernels: none -> 2.02 us  [shards(): pl.pallas_call(arrange, name='arrange', out_shape=(jax.ShapeDtypeStruct((...]
    pallas_call x1, Pallas kernels: 7.59 us -> 5.84 us  [shards(): pl.pallas_call(contract, name='contract', out_shape=jax.ShapeDtypeStruct(...]
    another operation x1 -> x0, other arithmetic: 0.65 us -> none  [shards(): me = jnp.stack([d * 2 + n, n]).astype(i32)]
    ppermute x3, starting transfers between devices: 5.9 us -> 5.3 us  [shards(): lax.ppermute(piece, 'draw', [(i, (i + shift) % 4) for i in range(4)])]
    all_to_all x1, blocking collectives: 13.4 us -> 12.8 us  [shards(): lax.all_to_all(results, ('draw', 'nest'), split_axis=0, concat_axis=0, ti...]
  transfers between devices with their start and end apart: 5 -> 5, of which waited for: 1 -> 1; matrix products, arithmetic and copies ran while one was open for 1% -> 0% of each run, Pallas kernels for 0% -> 4%
where the time goes in v2:
time: 52.2 us; the launch traced here: 51.6 us
  starting transfers between devices  17.7 us (34%)
  Pallas kernels  12.8 us (25%)
  blocking collectives  12.8 us (25%)
  local copies, waits for them, and re-layouts  4.5 us (9%)
  waiting for transfers between devices  3 us (6%)
  between operations  0.77 us (1%)
    all_to_all x1, blocking collectives, shards(): lax.all_to_all(results, ('draw', 'nest'), split_axis=0, concat_axis=0, ti...  12.8 us
    all_to_all x1, starting transfers between devices, shards(): recv = lax.all_to_all(send, 'mkt', split_axis=0, concat_axis=0, tiled=True)  10.2 us
    pallas_call x1, Pallas kernels, shards(): pl.pallas_call(contract, name='contract', out_shape=jax.ShapeDtypeStruct(...  5.84 us
    ppermute x3, starting transfers between devices, shards(): lax.ppermute(piece, 'draw', [(i, (i + shift) % 4) for i in range(4)])  5.3 us
    unnamed x18, local copies, waits for them, and re-layouts  4.32 us
    pallas_call x1, Pallas kernels, shards(): pl.pallas_call(pack, name='pack', out_shape=jax.ShapeDtypeStruct((BLOCKS,...  3.28 us
    ppermute x1, waiting for transfers between devices, shards(): far = lax.ppermute(near, 'nest', [(0, 1), (1, 0)])  2.99 us
    ppermute x1, starting transfers between devices, shards(): far = lax.ppermute(near, 'nest', [(0, 1), (1, 0)])  2.15 us
  transfers between devices with their start and end apart: 5, of which 1 were waited for; matrix products, arithmetic and copies ran while one was open for 0% of the time, Pallas kernels for 4%

profile of v2, /device:TPU:2, one launch (start us, length us, event | category | flops | bytes accessed | tf_op | source)
XLA Modules:
  0.0 51.6 jit_solution(5120061880752275200)
XLA Ops:
  0.6 3.3 %pack.1 = bf16[32,24,128]{2,1,0:T(8,128)(2,1)} custom-call(bf16[32,16,1024]{2,1,0:T(8,128)(2,1)} %f_ref.1, f32[16,1024]{1,0:T(8,128)} %l_ref.1), custom_call_target="tpu_custom_call" | custom-call | tf_op jit(solution)/shard_map/pack/pallas_call | solution.py:213
  3.9 0.0 copy-start.4
  3.9 10.2 %all-to-all-start = ((bf16[32,24,128]{2,1,0:T(8,128)(2,1)}), bf16[32,24,128]{2,1,0:T(8,128)(2,1)S(1)}, u32[]{:S(2)}, u32[]{:S(2)}) async-start(bf16[32,24,128]{2,1,0:T(8,128)(2,1)} %pack.1), calls=%async_computation | async-start | bytes 393216 | tf_op jit(solution)/shard_map/all_to_all | solution.py:225
  14.2 0.0 copy-done.4
  14.2 0.0 copy-start.8
  14.2 3.1 %collective-permute-start.2 = (bf16[4,32,128]{2,1,0:T(8,128)(2,1)S(1)}, bf16[4,32,128]{2,1,0:T(8,128)(2,1)S(1)}, u32[]{:S(2)}, u32[]{:S(2)}) collective-permute-start(bf16[4,32,128]{2,1,0:T(8,128)(2,1)S(1)} %get-tuple-element.10), channel_id=1, source_target_pairs={{0,6},{2,0},{4,2},{6,4},{1,7},{3,1},{5,3},{7,5},{8,14},{10,8},{12,... | collective-permute-start | bytes 98312 | tf_op jit(solution)/shard_map/ppermute | solution.py:251
  17.3 0.0 copy-start.6
  17.3 0.0 collective-permute-start
  17.3 2.2 %collective-permute-start.1 = (bf16[4,32,128]{2,1,0:T(8,128)(2,1)S(1)}, bf16[4,32,128]{2,1,0:T(8,128)(2,1)S(1)}, u32[]{:S(2)}, u32[]{:S(2)}) collective-permute-start(bf16[4,32,128]{2,1,0:T(8,128)(2,1)S(1)} %get-tuple-element.13), channel_id=1, source_target_pairs={{0,4},{2,6},{4,0},{6,2},{1,5},{3,7},{5,1},{7,3},{8,12},{10,14},{12... | collective-permute-start | bytes 98312 | tf_op jit(solution)/shard_map/ppermute | solution.py:251
  19.5 0.0 copy-done.8
  19.5 0.1 copy.8
  19.6 0.0 copy-done.6
  19.6 0.1 pad.2.clone
  19.7 0.1 maximum_maximum_fusion.near_ref
  19.8 0.0 copy-start.5
  19.8 2.1 %collective-permute-start.3 = (f32[8,128]{1,0:T(8,128)S(1)}, f32[8,128]{1,0:T(8,128)S(1)}, u32[]{:S(2)}, u32[]{:S(2)}) collective-permute-start(f32[8,128]{1,0:T(8,128)S(1)} %maximum_maximum_fusion.near_ref), channel_id=1, source_target_pairs={{0,1},{1,0},{2,3},{3,2},{4,5},{5,4},{6,7},{7,6},{8,9},{9,8},{10,11... | collective-permute-start | bytes 12296 | tf_op jit(solution)/shard_map/ppermute | solution.py:230
  21.9 3.0 %collective-permute-done.3.far_ref = f32[8,128]{1,0:T(8,128)S(1)} collective-permute-done((f32[8,128]{1,0:T(8,128)S(1)}, f32[8,128]{1,0:T(8,128)S(1)}, u32[]{:S(2)}, u32[]{:S(2)}) %collective-permute-start.3) | collective-permute-done | bytes 4128 | tf_op jit(solution)/shard_map/ppermute | solution.py:230
  24.9 0.0 copy-done.5
  24.9 0.6 %copy-done.7 = f32[8,128]{1,0:T(8,128)} copy-done((f32[8,128]{1,0:T(8,128)}, f32[8,128]{1,0:T(8,128)S(1)}, u32[]{:S(2)}) %copy-start.7) | copy-done | bytes 4120
  25.5 2.0 %arrange.1 = (f32[48,128]{1,0:T(8,128)}, bf16[768,512]{1,0:T(8,128)(2,1)}, bf16[768,128]{1,0:T(8,128)(2,1)}, bf16[768,128]{1,0:T(8,128)(2,1)}) custom-call(f32[8,128]{1,0:T(8,128)} %copy-done.5, f32[8,128]{1,0:T(8,128)} %copy-done.7, f32[1,32]{1,0:T(1,128)} %bitcast.5), custom_call_target="tpu_custom_call" | custom-call | flops 2000000 | bytes 2000000 | tf_op jit(solution)/shard_map/arrange/pallas_call | solution.py:232
  27.5 0.0 collective-permute-done.2.t3_ref
  27.5 0.0 collective-permute-done.t1_ref
  27.5 0.0 collective-permute-done.1.t2_ref
  27.6 0.0 all-to-all-done.x_ref
  27.6 0.0 copy-start
  27.6 1.1 %copy-done = bf16[768,512]{1,0:T(8,128)(2,1)S(1)} copy-done((bf16[768,512]{1,0:T(8,128)(2,1)S(1)}, bf16[768,512]{1,0:T(8,128)(2,1)}, u32[]{:S(2)}) %copy-start) | copy-done | bytes 786456
  28.7 0.9 %copy-done.1 = bf16[768,128]{1,0:T(8,128)(2,1)S(1)} copy-done((bf16[768,128]{1,0:T(8,128)(2,1)S(1)}, bf16[768,128]{1,0:T(8,128)(2,1)}, u32[]{:S(2)}) %copy-start.1) | copy-done | bytes 196632
  29.6 0.9 %copy-done.2 = bf16[768,128]{1,0:T(8,128)(2,1)S(1)} copy-done((bf16[768,128]{1,0:T(8,128)(2,1)S(1)}, bf16[768,128]{1,0:T(8,128)(2,1)}, u32[]{:S(2)}) %copy-start.2) | copy-done | bytes 196632
  30.6 0.7 %copy-done.3 = f32[48,128]{1,0:T(8,128)S(1)} copy-done((f32[48,128]{1,0:T(8,128)S(1)}, f32[48,128]{1,0:T(8,128)}, u32[]{:S(2)}) %copy-start.3) | copy-done | bytes 24600
  31.3 5.8 %contract.1 = f32[8,32,128]{2,1,0:T(8,128)S(1)} custom-call(bf16[32,24,128]{2,1,0:T(8,128)(2,1)S(1)} %all-to-all-done.x_ref, bf16[4,32,128]{2,1,0:T(8,128)(2,1)S(1)} %get-tuple-element.12.t0_ref, bf16[4,32,128]{2,1,0:T(8,128)(2,1)S(1)} %collective-permute-done.t1_ref, bf16[4,32,128]{2,1,0:T(8,128)(2,1)S(1)} %collective-permute-done.1.t2_ref, ...), custom_call_target="tpu_custom_call" | custom-call | tf_op jit(solution)/shard_map/contract/pallas_call | solution.py:256
  37.1 12.8 %all_to_all.10 = f32[8,32,128]{2,1,0:T(8,128)} all-to-all(f32[8,32,128]{2,1,0:T(8,128)S(1)} %contract.1), channel_id=1, replica_groups=mesh['mkt'=32,'draw'=4,'nest'=2] {'draw','nest'}, dimensions={0} | all-to-all | bytes 262144 | tf_op jit(solution)/shard_map/all_to_all | solution.py:273
  50.0 1.7 %unpack.1 = (f32[32,384]{1,0:T(8,128)}, f32[32,384]{1,0:T(8,128)}) custom-call(f32[256,128]{1,0:T(8,128)} %bitcast.3), custom_call_target="tpu_custom_call" | custom-call | tf_op jit(solution)/shard_map/unpack/pallas_call | solution.py:275
  (7 shorter events, 0.0 us)
Async XLA Ops:
  3.9 10.3 %copy-start.4 = (bf16[32,32,128]{2,1,0:T(8,128)(2,1)S(1)}, bf16[32,32,128]{2,1,0:T(8,128)(2,1)}, u32[]{:S(2)}) copy-start(bf16[32,32,128]{2,1,0:T(8,128)(2,1)} %param.7) | copy-start | bytes 786436
  3.9 23.6 %all-to-all-start = ((bf16[32,24,128]{2,1,0:T(8,128)(2,1)}), bf16[32,24,128]{2,1,0:T(8,128)(2,1)S(1)}, u32[]{:S(2)}, u32[]{:S(2)}) async-start(bf16[32,24,128]{2,1,0:T(8,128)(2,1)} %pack.1), calls=%async_computation | async-start | bytes 393216 | tf_op jit(solution)/shard_map/all_to_all | solution.py:225
  14.2 5.3 %copy-start.8 = (f32[8]{0:T(128)S(1)}, f32[8]{0:T(128)}, u32[]{:S(2)}) copy-start(f32[8]{0:T(128)} %param.9) | copy-start | bytes 100
  14.2 13.3 %collective-permute-start.2 = (bf16[4,32,128]{2,1,0:T(8,128)(2,1)S(1)}, bf16[4,32,128]{2,1,0:T(8,128)(2,1)S(1)}, u32[]{:S(2)}, u32[]{:S(2)}) collective-permute-start(bf16[4,32,128]{2,1,0:T(8,128)(2,1)S(1)} %get-tuple-element.10), channel_id=1, source_target_pairs={{0,6},{2,0},{4,2},{6,4},{1,7},{3,1},{5,3},{7,5},{8,14},{10,8},{12,... | collective-permute-start | bytes 98312 | tf_op jit(solution)/shard_map/ppermute | solution.py:251
  17.3 2.3 %copy-start.6 = (s32[8,48]{1,0:T(8,128)S(1)}, s32[8,48]{1,0:T(8,128)}, u32[]{:S(2)}) copy-start(s32[8,48]{1,0:T(8,128)} %param.10) | copy-start | bytes 4612
  17.3 10.2 %collective-permute-start = (bf16[4,32,128]{2,1,0:T(8,128)(2,1)S(1)}, bf16[4,32,128]{2,1,0:T(8,128)(2,1)S(1)}, u32[]{:S(2)}, u32[]{:S(2)}) collective-permute-start(bf16[4,32,128]{2,1,0:T(8,128)(2,1)S(1)} %get-tuple-element.11), channel_id=1, source_target_pairs={{0,2},{2,4},{4,6},{6,0},{1,3},{3,5},{5,7},{7,1},{8,10},{10,12},{12... | collective-permute-start | bytes 98312 | tf_op jit(solution)/shard_map/ppermute | solution.py:251
  17.3 10.2 %collective-permute-start.1 = (bf16[4,32,128]{2,1,0:T(8,128)(2,1)S(1)}, bf16[4,32,128]{2,1,0:T(8,128)(2,1)S(1)}, u32[]{:S(2)}, u32[]{:S(2)}) collective-permute-start(bf16[4,32,128]{2,1,0:T(8,128)(2,1)S(1)} %get-tuple-element.13), channel_id=1, source_target_pairs={{0,4},{2,6},{4,0},{6,2},{1,5},{3,7},{5,1},{7,3},{8,12},{10,14},{12... | collective-permute-start | bytes 98312 | tf_op jit(solution)/shard_map/ppermute | solution.py:251
  19.8 5.1 %copy-start.5 = (f32[8,128]{1,0:T(8,128)}, f32[8,128]{1,0:T(8,128)S(1)}, u32[]{:S(2)}) copy-start(f32[8,128]{1,0:T(8,128)S(1)} %maximum_maximum_fusion.near_ref) | copy-start | bytes 12292
  19.8 5.1 %collective-permute-start.3 = (f32[8,128]{1,0:T(8,128)S(1)}, f32[8,128]{1,0:T(8,128)S(1)}, u32[]{:S(2)}, u32[]{:S(2)}) collective-permute-start(f32[8,128]{1,0:T(8,128)S(1)} %maximum_maximum_fusion.near_ref), channel_id=1, source_target_pairs={{0,1},{1,0},{2,3},{3,2},{4,5},{5,4},{6,7},{7,6},{8,9},{9,8},{10,11... | collective-permute-start | bytes 12296 | tf_op jit(solution)/shard_map/ppermute | solution.py:230
  24.9 0.6 %copy-start.7 = (f32[8,128]{1,0:T(8,128)}, f32[8,128]{1,0:T(8,128)S(1)}, u32[]{:S(2)}) copy-start(f32[8,128]{1,0:T(8,128)S(1)} %collective-permute-done.3.far_ref) | copy-start | bytes 12292
  27.6 1.1 %copy-start = (bf16[768,512]{1,0:T(8,128)(2,1)S(1)}, bf16[768,512]{1,0:T(8,128)(2,1)}, u32[]{:S(2)}) copy-start(bf16[768,512]{1,0:T(8,128)(2,1)} %get-tuple-element.7.hot_ref) | copy-start | bytes 2359300
  28.7 0.9 %copy-start.1 = (bf16[768,128]{1,0:T(8,128)(2,1)S(1)}, bf16[768,128]{1,0:T(8,128)(2,1)}, u32[]{:S(2)}) copy-start(bf16[768,128]{1,0:T(8,128)(2,1)} %get-tuple-element.8.pick_ref) | copy-start | bytes 589828
  29.6 0.9 %copy-start.2 = (bf16[768,128]{1,0:T(8,128)(2,1)S(1)}, bf16[768,128]{1,0:T(8,128)(2,1)}, u32[]{:S(2)}) copy-start(bf16[768,128]{1,0:T(8,128)(2,1)} %get-tuple-element.9.mask_ref) | copy-start | bytes 589828
  30.6 0.7 %copy-start.3 = (f32[48,128]{1,0:T(8,128)S(1)}, f32[48,128]{1,0:T(8,128)}, u32[]{:S(2)}) copy-start(f32[48,128]{1,0:T(8,128)} %get-tuple-element.6.table_ref) | copy-start | bytes 73732

commit v3 on v2

--- a/solution.py
+++ b/solution.py
@@ -1,4 +1,3 @@
-import functools
 import math
 
 import jax
@@ -7,6 +6,7 @@
 from jax.experimental import pallas as pl
 from jax.experimental.pallas import tpu as pltpu
 from jax.sharding import PartitionSpec as P
+
 
 ITERS = 3
 BLOCKS = 32
@@ -22,11 +22,14 @@
 ROWS = 24
 LOG2E = 1.0 / math.log(2.0)
 LOW = -1e30
+MIB = 1024 * 1024
 TINY = 1.1754944e-38
 EMPTY = 32 * 16 + 15
 PLACES = [(o, t) for o in range(2) for t in range(SLOTS)]
 f32, bf16, i32 = jnp.float32, jnp.bfloat16, jnp.int32
 VMEM = pl.BlockSpec(memory_space=pltpu.VMEM)
+HBM = pl.BlockSpec(memory_space=pltpu.HBM)
+PARTS = 2
 
 
 def iota(shape, dim):
@@ -41,32 +44,58 @@
     return lax.dot_general(a, b, (((1,), (1,)), ((), ())), preferred_element_type=f32)
 
 
-def pack(f_ref, l_ref, out_ref, g_ref, o_ref, s_ref):
+def pack(f_hbm, l_hbm, out_hbm, f_ref, l_ref, g_ref, o_ref, s_ref, out_ref, sems):
+    loads = [pltpu.make_async_copy(l_hbm, l_ref, sems.at[PARTS])]
+    for c in range(PARTS):
+        part = pl.ds(c * K // PARTS, K // PARTS)
+        loads.append(pltpu.make_async_copy(f_hbm.at[part], f_ref.at[part], sems.at[c]))
+    for load in loads:
+        load.start()
     base = (lax.axis_index("draw") * 2 + lax.axis_index("nest")) * QUAD
     market = iota((MARKETS, LANES), 0)
     lane = iota((MARKETS, LANES), 1)
     pick = jnp.where(market == (lane % BLOCKS) * 32 + base + lane // BLOCKS, 1.0, 0.0).astype(bf16)
-    g_ref[...] = dot(f_ref[...].reshape(K * PROD, MARKETS), pick)
+    spread = jnp.where(iota((BLOCKS, LANES), 0) == iota((BLOCKS, LANES), 1) % BLOCKS, 1.0, 0.0).astype(bf16)
+
+    loads[0].wait()
     log = l_ref[...]
     high = log.astype(bf16)
     rest = log - high.astype(f32)
     middle = rest.astype(bf16)
     low = (rest - middle.astype(f32)).astype(bf16)
     logs = dot(jnp.concatenate([high, middle, low], axis=0), pick)
-    spread = jnp.where(iota((BLOCKS, LANES), 0) == iota((BLOCKS, LANES), 1) % BLOCKS, 1.0, 0.0).astype(bf16)
-    own = iota((LANES, LANES), 0) // K == iota((LANES, LANES), 1) // BLOCKS
-    for j in range(PROD):
-        part = g_ref[pl.ds(j, K, stride=PROD), :]
-        part = jnp.where(own, jnp.concatenate([part] * QUAD, axis=0), 0.0).astype(bf16)
-        o_ref[pl.ds(j, BLOCKS, stride=PROD), :] = dot_t(spread, part)
-    out_ref[:, :PROD, :] = o_ref[...].reshape(BLOCKS, PROD, LANES).astype(bf16)
     own = (iota((LANES, LANES), 0) // PROD) % QUAD == iota((LANES, LANES), 1) // BLOCKS
     first = jnp.concatenate([logs[:PROD]] * QUAD + [logs[PROD : 2 * PROD]] * QUAD, axis=0)
     second = jnp.concatenate([logs[2 * PROD :]] * QUAD + [jnp.zeros((64, LANES), f32)], axis=0)
     s_ref[...] = jnp.zeros_like(s_ref)
     s_ref[pl.ds(0, BLOCKS, stride=8), :] = dot_t(spread, jnp.where(own, first, 0.0).astype(bf16))
     s_ref[pl.ds(1, BLOCKS, stride=8), :] = dot_t(spread, jnp.where(own, second, 0.0).astype(bf16))
-    out_ref[:, PROD:, :] = s_ref[...].reshape(BLOCKS, 8, LANES).astype(bf16)
+
+    rows = K * PROD // PARTS
+    for c in range(PARTS):
+        loads[1 + c].wait()
+        part = f_ref[c * K // PARTS : (c + 1) * K // PARTS].reshape(rows, MARKETS)
+        g_ref[c * rows : (c + 1) * rows, :] = dot(part, pick)
+    own = iota((LANES, LANES), 0) // K == iota((LANES, LANES), 1) // BLOCKS
+    parts = []
+    for j in range(PROD):
+        part = g_ref[pl.ds(j, K, stride=PROD), :]
+        parts.append(jnp.where(own, jnp.concatenate([part] * QUAD, axis=0), 0.0).astype(bf16))
+    goods = dot_t(spread, jnp.concatenate(parts, axis=0))
+    for j in range(PROD):
+        o_ref[pl.ds(j, BLOCKS, stride=PROD), :] = goods[:, j * LANES : (j + 1) * LANES]
+    stores = []
+    for c in range(2):
+        half = slice(c * BLOCKS // 2, (c + 1) * BLOCKS // 2)
+        goods = o_ref[c * 256 : (c + 1) * 256, :].reshape(BLOCKS // 2, PROD, LANES)
+        out_ref[half, :PROD, :] = goods.astype(bf16)
+        logs = s_ref[c * 128 : (c + 1) * 128, :].reshape(BLOCKS // 2, 8, LANES)
+        out_ref[half, PROD:, :] = logs.astype(bf16)
+        half = pl.ds(c * BLOCKS // 2, BLOCKS // 2)
+        stores.append(pltpu.make_async_copy(out_ref.at[half], out_hbm.at[half], sems.at[c]))
+        stores[-1].start()
+    for store in stores:
+        store.wait()
 
 
 def across(x):
@@ -214,12 +243,16 @@
         pack,
         name="pack",
         out_shape=jax.ShapeDtypeStruct((BLOCKS, ROWS, LANES), bf16),
-        in_specs=[VMEM, VMEM],
-        out_specs=VMEM,
+        in_specs=[HBM, HBM],
+        out_specs=HBM,
         scratch_shapes=[
+            pltpu.VMEM((K, PROD, MARKETS), bf16),
+            pltpu.VMEM((PROD, MARKETS), f32),
             pltpu.VMEM((K * PROD, LANES), f32),
             pltpu.VMEM((BLOCKS * PROD, LANES), f32),
             pltpu.VMEM((BLOCKS * 8, LANES), f32),
+            pltpu.VMEM((BLOCKS, ROWS, LANES), bf16),
+            pltpu.SemaphoreType.DMA((PARTS + 1,)),
         ],
     )(features, log_share)
     recv = lax.all_to_all(send, "mkt", split_axis=0, concat_axis=0, tiled=True)
@@ -241,6 +274,7 @@
         in_specs=[VMEM] * 3,
         out_specs=(VMEM,) * 4,
         cost_estimate=pl.CostEstimate(flops=2_000_000, bytes_accessed=2_000_000, transcendentals=0),
+        compiler_params=pltpu.CompilerParams(vmem_limit_bytes=4 * MIB),
     )(near, far, taste_scale.reshape(1, K))
     d, n = lax.axis_index("draw"), lax.axis_index("nest")
     tastes = []
@@ -268,12 +302,17 @@
             pltpu.VMEM(small, f32),
             pltpu.VMEM((BLOCKS * 8, LANES), f32),
         ],
-        compiler_params=pltpu.CompilerParams(vmem_limit_bytes=40 * 1024 * 1024),
+        compiler_params=pltpu.CompilerParams(vmem_limit_bytes=36 * MIB),
     )(recv, *tastes, *plan)
     gathered = lax.all_to_all(results, ("draw", "nest"), split_axis=0, concat_axis=0, tiled=True)
     shape = jax.ShapeDtypeStruct((32, HALF * SLOTS), f32)
     return pl.pallas_call(
-        unpack, name="unpack", out_shape=(shape, shape), in_specs=[VMEM], out_specs=(VMEM, VMEM)
+        unpack,
+        name="unpack",
+        out_shape=(shape, shape),
+        in_specs=[VMEM],
+        out_specs=(VMEM, VMEM),
+        compiler_params=pltpu.CompilerParams(vmem_limit_bytes=2 * MIB),
     )(gathered.reshape(256, LANES))
 
 
@@ -287,4 +326,6 @@
         P("mkt", None),
     )
     out_specs = (P("mkt", "nest"), P("mkt", "nest"))
+
+
     return jax.shard_map(shards, mesh=mesh, in_specs=in_specs, out_specs=out_specs, check_vma=False)

time: 52.2 us -> 45.1 us (0.86)
  local copies, waits for them, and re-layouts: 4.5 us -> 0.2 us
  Pallas kernels: 12.8 us -> 9.62 us
  blocking collectives: 12.8 us -> 13.5 us
    unnamed x18 -> x8, local copies, waits for them, and re-layouts: 4.32 us -> 0.02 us
    pallas_call x1, Pallas kernels: 2.02 us -> 0.31 us  [shards(): pl.pallas_call(arrange, name='arrange', out_shape=(jax.ShapeDtypeStruct((...]
    pallas_call x1, Pallas kernels: 1.66 us -> 0.76 us  [shards(): pl.pallas_call(unpack, name='unpack', out_shape=(shape, shape), in_specs=...]
    all_to_all x1, blocking collectives: 12.8 us -> 13.5 us  [shards(): lax.all_to_all(results, ('draw', 'nest'), split_axis=0, concat_axis=0, ti...]
    pallas_call x1, Pallas kernels: 3.28 us -> 2.71 us  [shards(): pl.pallas_call(pack, name='pack', out_shape=jax.ShapeDtypeStruct((BLOCKS,...]
  transfers between devices with their start and end apart: 5 -> 5, of which waited for: 1 -> 1; matrix products, arithmetic and copies ran while one was open for 0% -> 1% of each run, Pallas kernels for 4% -> 1%
where the time goes in v3:
time: 45.1 us; the launch traced here: 44.9 us
  starting transfers between devices  17.7 us (39%)
  blocking collectives  13.5 us (30%)
  Pallas kernels  9.62 us (21%)
  waiting for transfers between devices  2.99 us (7%)
  between operations  0.79 us (2%)
    all_to_all x1, blocking collectives, shards(): lax.all_to_all(results, ('draw', 'nest'), split_axis=0, concat_axis=0, ti...  13.5 us
    all_to_all x1, starting transfers between devices, shards(): recv = lax.all_to_all(send, 'mkt', split_axis=0, concat_axis=0, tiled=True)  10.2 us
    pallas_call x1, Pallas kernels, shards(): pl.pallas_call(contract, name='contract', out_shape=jax.ShapeDtypeStruct(...  5.83 us
    ppermute x3, starting transfers between devices, shards(): lax.ppermute(piece, 'draw', [(i, (i + shift) % 4) for i in range(4)])  5.3 us
    ppermute x1, waiting for transfers between devices, shards(): far = lax.ppermute(near, 'nest', [(0, 1), (1, 0)])  2.98 us
    pallas_call x1, Pallas kernels, shards(): pl.pallas_call(pack, name='pack', out_shape=jax.ShapeDtypeStruct((BLOCKS,...  2.71 us
    ppermute x1, starting transfers between devices, shards(): far = lax.ppermute(near, 'nest', [(0, 1), (1, 0)])  2.16 us
  transfers between devices with their start and end apart: 5, of which 1 were waited for; matrix products, arithmetic and copies ran while one was open for 1% of the time, Pallas kernels for 1%

profile of v3, /device:TPU:2, one launch (start us, length us, event | category | flops | bytes accessed | tf_op | source)
XLA Modules:
  0.0 44.9 jit_solution(10444692249003563727)
XLA Ops:
  0.6 2.7 %pack.1 = bf16[32,24,128]{2,1,0:T(8,128)(2,1)} custom-call(bf16[32,16,1024]{2,1,0:T(8,128)(2,1)} %f_hbm.1, f32[16,1024]{1,0:T(8,128)} %l_hbm.1), custom_call_target="tpu_custom_call" | custom-call | tf_op jit(solution)/shard_map/pack/pallas_call | solution.py:242
  3.4 0.0 copy-start.1
  3.4 10.2 %all-to-all-start = ((bf16[32,24,128]{2,1,0:T(8,128)(2,1)}), bf16[32,24,128]{2,1,0:T(8,128)(2,1)S(1)}, u32[]{:S(2)}, u32[]{:S(2)}) async-start(bf16[32,24,128]{2,1,0:T(8,128)(2,1)} %pack.1), calls=%async_computation | async-start | bytes 393216 | tf_op jit(solution)/shard_map/all_to_all | solution.py:258
  13.7 0.0 copy-done.1
  13.7 0.0 copy-start.3
  13.7 3.1 %collective-permute-start.2 = (bf16[4,32,128]{2,1,0:T(8,128)(2,1)S(1)}, bf16[4,32,128]{2,1,0:T(8,128)(2,1)S(1)}, u32[]{:S(2)}, u32[]{:S(2)}) collective-permute-start(bf16[4,32,128]{2,1,0:T(8,128)(2,1)S(1)} %get-tuple-element.10), channel_id=1, source_target_pairs={{0,6},{2,0},{4,2},{6,4},{1,7},{3,1},{5,3},{7,5},{8,14},{10,8},{12,... | collective-permute-start | bytes 98312 | tf_op jit(solution)/shard_map/ppermute | solution.py:285
  16.8 0.0 copy-start.2
  16.8 0.0 collective-permute-start
  16.8 2.2 %collective-permute-start.1 = (bf16[4,32,128]{2,1,0:T(8,128)(2,1)S(1)}, bf16[4,32,128]{2,1,0:T(8,128)(2,1)S(1)}, u32[]{:S(2)}, u32[]{:S(2)}) collective-permute-start(bf16[4,32,128]{2,1,0:T(8,128)(2,1)S(1)} %get-tuple-element.13), channel_id=1, source_target_pairs={{0,4},{2,6},{4,0},{6,2},{1,5},{3,7},{5,1},{7,3},{8,12},{10,14},{12... | collective-permute-start | bytes 98312 | tf_op jit(solution)/shard_map/ppermute | solution.py:285
  19.0 0.0 copy-done.3
  19.0 0.1 copy.8
  19.1 0.0 copy-done.2
  19.1 0.1 pad.2.clone
  19.2 0.1 maximum_maximum_fusion.near_ref
  19.3 0.0 copy-start
  19.3 2.2 %collective-permute-start.3 = (f32[8,128]{1,0:T(8,128)S(1)}, f32[8,128]{1,0:T(8,128)S(1)}, u32[]{:S(2)}, u32[]{:S(2)}) collective-permute-start(f32[8,128]{1,0:T(8,128)S(1)} %maximum_maximum_fusion.near_ref), channel_id=1, source_target_pairs={{0,1},{1,0},{2,3},{3,2},{4,5},{5,4},{6,7},{7,6},{8,9},{9,8},{10,11... | collective-permute-start | bytes 12296 | tf_op jit(solution)/shard_map/ppermute | solution.py:263
  21.4 3.0 %collective-permute-done.3.far_ref = f32[8,128]{1,0:T(8,128)S(1)} collective-permute-done((f32[8,128]{1,0:T(8,128)S(1)}, f32[8,128]{1,0:T(8,128)S(1)}, u32[]{:S(2)}, u32[]{:S(2)}) %collective-permute-start.3) | collective-permute-done | bytes 4128 | tf_op jit(solution)/shard_map/ppermute | solution.py:263
  24.4 0.0 copy-done
  24.4 0.3 arrange.1
  24.7 0.0 collective-permute-done.2.t3_ref
  24.7 0.0 collective-permute-done.t1_ref
  24.7 0.0 collective-permute-done.1.t2_ref
  24.7 0.0 all-to-all-done.x_ref
  24.8 5.8 %contract.1 = f32[8,32,128]{2,1,0:T(8,128)S(1)} custom-call(bf16[32,24,128]{2,1,0:T(8,128)(2,1)S(1)} %all-to-all-done.x_ref, bf16[4,32,128]{2,1,0:T(8,128)(2,1)S(1)} %get-tuple-element.12.t0_ref, bf16[4,32,128]{2,1,0:T(8,128)(2,1)S(1)} %collective-permute-done.t1_ref, bf16[4,32,128]{2,1,0:T(8,128)(2,1)S(1)} %collective-permute-done.1.t2_ref, ...), custom_call_target="tpu_custom_call" | custom-call | tf_op jit(solution)/shard_map/contract/pallas_call | solution.py:290
  30.6 13.5 %all_to_all.10 = f32[8,32,128]{2,1,0:T(8,128)S(1)} all-to-all(f32[8,32,128]{2,1,0:T(8,128)S(1)} %contract.1), channel_id=1, replica_groups=mesh['mkt'=32,'draw'=4,'nest'=2] {'draw','nest'}, dimensions={0} | all-to-all | bytes 262144 | tf_op jit(solution)/shard_map/all_to_all | solution.py:307
  44.1 0.8 %unpack.1 = (f32[32,384]{1,0:T(8,128)}, f32[32,384]{1,0:T(8,128)}) custom-call(f32[256,128]{1,0:T(8,128)S(1)} %bitcast.3), custom_call_target="tpu_custom_call" | custom-call | tf_op jit(solution)/shard_map/unpack/pallas_call | solution.py:309
  (3 shorter events, 0.0 us)
Async XLA Ops:
  3.4 10.3 %copy-start.1 = (bf16[32,32,128]{2,1,0:T(8,128)(2,1)S(1)}, bf16[32,32,128]{2,1,0:T(8,128)(2,1)}, u32[]{:S(2)}) copy-start(bf16[32,32,128]{2,1,0:T(8,128)(2,1)} %param.7) | copy-start | bytes 786436
  3.4 21.4 %all-to-all-start = ((bf16[32,24,128]{2,1,0:T(8,128)(2,1)}), bf16[32,24,128]{2,1,0:T(8,128)(2,1)S(1)}, u32[]{:S(2)}, u32[]{:S(2)}) async-start(bf16[32,24,128]{2,1,0:T(8,128)(2,1)} %pack.1), calls=%async_computation | async-start | bytes 393216 | tf_op jit(solution)/shard_map/all_to_all | solution.py:258
  13.7 5.3 %copy-start.3 = (f32[8]{0:T(128)S(1)}, f32[8]{0:T(128)}, u32[]{:S(2)}) copy-start(f32[8]{0:T(128)} %param.9) | copy-start | bytes 100
  13.7 11.0 %collective-permute-start.2 = (bf16[4,32,128]{2,1,0:T(8,128)(2,1)S(1)}, bf16[4,32,128]{2,1,0:T(8,128)(2,1)S(1)}, u32[]{:S(2)}, u32[]{:S(2)}) collective-permute-start(bf16[4,32,128]{2,1,0:T(8,128)(2,1)S(1)} %get-tuple-element.10), channel_id=1, source_target_pairs={{0,6},{2,0},{4,2},{6,4},{1,7},{3,1},{5,3},{7,5},{8,14},{10,8},{12,... | collective-permute-start | bytes 98312 | tf_op jit(solution)/shard_map/ppermute | solution.py:285
  16.8 2.3 %copy-start.2 = (s32[8,48]{1,0:T(8,128)S(1)}, s32[8,48]{1,0:T(8,128)}, u32[]{:S(2)}) copy-start(s32[8,48]{1,0:T(8,128)} %param.10) | copy-start | bytes 4612
  16.8 7.9 %collective-permute-start = (bf16[4,32,128]{2,1,0:T(8,128)(2,1)S(1)}, bf16[4,32,128]{2,1,0:T(8,128)(2,1)S(1)}, u32[]{:S(2)}, u32[]{:S(2)}) collective-permute-start(bf16[4,32,128]{2,1,0:T(8,128)(2,1)S(1)} %get-tuple-element.11), channel_id=1, source_target_pairs={{0,2},{2,4},{4,6},{6,0},{1,3},{3,5},{5,7},{7,1},{8,10},{10,12},{12... | collective-permute-start | bytes 98312 | tf_op jit(solution)/shard_map/ppermute | solution.py:285
  16.8 7.9 %collective-permute-start.1 = (bf16[4,32,128]{2,1,0:T(8,128)(2,1)S(1)}, bf16[4,32,128]{2,1,0:T(8,128)(2,1)S(1)}, u32[]{:S(2)}, u32[]{:S(2)}) collective-permute-start(bf16[4,32,128]{2,1,0:T(8,128)(2,1)S(1)} %get-tuple-element.13), channel_id=1, source_target_pairs={{0,4},{2,6},{4,0},{6,2},{1,5},{3,7},{5,1},{7,3},{8,12},{10,14},{12... | collective-permute-start | bytes 98312 | tf_op jit(solution)/shard_map/ppermute | solution.py:285
  19.3 5.1 %copy-start = (f32[32]{0:T(128)S(1)}, f32[32]{0:T(128)}, u32[]{:S(2)}) copy-start(f32[32]{0:T(128)} %param.8) | copy-start | bytes 388
  19.3 5.1 %collective-permute-start.3 = (f32[8,128]{1,0:T(8,128)S(1)}, f32[8,128]{1,0:T(8,128)S(1)}, u32[]{:S(2)}, u32[]{:S(2)}) collective-permute-start(f32[8,128]{1,0:T(8,128)S(1)} %maximum_maximum_fusion.near_ref), channel_id=1, source_target_pairs={{0,1},{1,0},{2,3},{3,2},{4,5},{5,4},{6,7},{7,6},{8,9},{9,8},{10,11... | collective-permute-start | bytes 12296 | tf_op jit(solution)/shard_map/ppermute | solution.py:263

commit v4 on v3

--- a/solution.py
+++ b/solution.py
@@ -25,7 +25,9 @@
 MIB = 1024 * 1024
 TINY = 1.1754944e-38
 EMPTY = 32 * 16 + 15
-PLACES = [(o, t) for o in range(2) for t in range(SLOTS)]
+CUT = 32
+PLACES = [(o, t) for t in range(CUT) for o in range(2)] + [(o, t) for o in range(2) for t in range(CUT, SLOTS)]
+SHORT = len(PLACES) - (SLOTS - CUT)
 f32, bf16, i32 = jnp.float32, jnp.bfloat16, jnp.int32
 VMEM = pl.BlockSpec(memory_space=pltpu.VMEM)
 HBM = pl.BlockSpec(memory_space=pltpu.HBM)
@@ -106,10 +108,25 @@
     near, far = near_ref[...], far_ref[...]
     first = lax.axis_index("nest") == 0
     table = jnp.concatenate([jnp.where(first, near, far), jnp.where(first, far, near)], axis=0)
+    row, lane = iota((NESTS, LANES), 0), iota((NESTS, LANES), 1)
+    filled = jnp.where((lane < SLOTS) & (table >= 0.0), 1.0, 0.0)
+    size = jnp.broadcast_to(jnp.sum(filled, axis=1, keepdims=True), (NESTS, LANES))
+    across_size = jnp.sum(jnp.where(row == lane, size, 0.0), axis=0, keepdims=True)
+    ahead = (across_size > size) | ((across_size == size) & (lane < row))
+    ahead = jnp.where(ahead & (lane < NESTS), 1.0, 0.0)
+    rank = jnp.broadcast_to(jnp.sum(ahead, axis=1, keepdims=True), (NESTS, LANES))
+    across_rank = jnp.sum(jnp.where(row == lane, rank, 0.0), axis=0, keepdims=True)
+    place = jnp.where((across_rank == row.astype(f32)) & (lane < NESTS), 1.0, 0.0)
+    ordered = table
+    for g in range(NESTS):
+        chosen = jnp.broadcast_to(place[:, g : g + 1], (NESTS, LANES)) > 0.5
+        ordered = jnp.where(chosen, jnp.broadcast_to(table[g : g + 1, :], (NESTS, LANES)), ordered)
+    table = ordered
     table_ref[:NESTS, :] = table
+    table_ref[NESTS + K :, :] = rank
     square = iota((K, K), 0) == iota((K, K), 1)
     scale = jnp.sum(jnp.where(square, jnp.broadcast_to(scale_ref[...], (K, K)), 0.0), axis=1, keepdims=True)
-    table_ref[NESTS:, :] = jnp.broadcast_to(scale, (K, LANES))
+    table_ref[NESTS : NESTS + K, :] = jnp.broadcast_to(scale, (K, LANES))
     ids = table.astype(i32)
     ids = jnp.where(ids < 0, EMPTY, ids)
     wide, narrow = iota((HALF, DRAWS), 1), iota((HALF, LANES), 1)
@@ -126,14 +143,14 @@
         mask_ref[rows, :] = jnp.concatenate(mask, axis=0).astype(bf16)
 
 
-def contract(x_ref, t0_ref, t1_ref, t2_ref, t3_ref, table_ref, hot_ref, pick_ref, mask_ref, out_ref,
-             slot_ref, taste_ref, mu_ref, e_ref, v_ref, t_ref, l_ref):
+def solve(count, x_ref, taste_refs, table_ref, hot_ref, pick_ref, mask_ref, out_ref, slot_ref, taste_ref, l_ref):
+    used = count * HALF
     table = [table_ref[o * HALF : (o + 1) * HALF, :] for o in range(2)]
     rate = [jnp.broadcast_to(x[:, SLOTS : SLOTS + 1], (HALF, LANES)) for x in table]
     inverse = [1.0 / x for x in rate]
     to_two = [across(LOG2E * x) for x in inverse]
-    gain = [(1.0 - x) * y for x, y in zip(rate, inverse)]
-    less = [across(x - 1.0) for x in rate]
+    gain = [(1.0 - x) * y[:, :LANES] for x, y in zip(rate, to_two)]
+    less = [across((x - 1.0) * LOG2E) for x in rate]
     narrow = iota((HALF, LANES), 1)
 
     l_ref[...] = x_ref[:, PROD:, :].astype(f32).reshape(BLOCKS * 8, LANES)
@@ -143,13 +160,16 @@
     lane = iota((BLOCKS, 2 * LANES), 1)
     lows = (iota((BLOCKS, 2 * LANES), 0) == 0) & (lane < 64) & (lane % PROD == PROD - 1)
     both = jnp.concatenate([both, jnp.where(lows, LOW, 0.0), jnp.zeros((64, 2 * LANES), f32)], axis=0).astype(bf16)
-    rows = dot(pick_ref[...], both).astype(bf16)
-    mask = mask_ref[...]
+    rows = dot(pick_ref[:used, :], both).astype(bf16)
+    mask = mask_ref[:used, :]
     rows = rows * jnp.concatenate([mask, mask], axis=1)
-    copies = jnp.where(
-        (iota((2 * LANES, DRAWS), 0) // PROD) % QUAD == iota((2 * LANES, DRAWS), 1) // LANES, 1.0, 0.0
-    ).astype(bf16)
-    target = dot(rows, copies)
+    source, lane = iota((2 * LANES, LANES), 0), iota((2 * LANES, LANES), 1)
+    fold = jnp.where((source // 64) * QUAD + (source // PROD) % QUAD == lane, 1.0, 0.0).astype(bf16)
+    parts = dot(rows, fold)
+    ones = jnp.where((narrow >= 3 * QUAD) & (narrow < 3 * QUAD + 3), 1.0, 0.0)
+    slot_ref[:used, LANES:] = (parts + jnp.concatenate([ones] * count, axis=0)).astype(bf16)
+    copies = jnp.where((source // PROD) % QUAD == lane // 32, 1.0, 0.0).astype(bf16)
+    goals = dot(rows, copies)
     whole = (top + pltpu.roll(top, 64, 1)) + rest
     shares = jnp.exp(whole)
     column = iota((BLOCKS, LANES), 1)
@@ -157,78 +177,114 @@
     for q in range(QUAD):
         inside = jnp.where(column // PROD == q, shares, 0.0)
         total = 1.0 - jnp.sum(jnp.sum(inside, axis=1, keepdims=True), axis=0, keepdims=True)
-        outside.append(lax.log2(jnp.broadcast_to(total, (HALF, LANES))))
+        outside.append(jnp.log(jnp.broadcast_to(total, (NESTS, LANES))))
 
     x = x_ref[:, :PROD, :].reshape(BLOCKS * PROD, LANES)
-    slot_ref[...] = dot(hot_ref[...], x).astype(bf16)
-    scale = table_ref[NESTS:, :]
+    slot_ref[:used, :LANES] = dot(hot_ref[:used, :], x).astype(bf16)
+    scale = table_ref[NESTS : NESTS + K, :]
     taste_ref[...] = jnp.zeros_like(taste_ref)
     for q in range(QUAD):
-        for b, ref in enumerate((t0_ref, t1_ref, t2_ref, t3_ref)):
+        for b, ref in enumerate(taste_refs):
             taste = (scale * ref[q].astype(f32)).astype(bf16)
             taste_ref[q, q * K : (q + 1) * K, b * LANES : (b + 1) * LANES] = taste
+        row = iota((NESTS, LANES), 0)
+        start = jnp.where((row < 3 * QUAD) & (row % QUAD == q), 1.0, 0.0)
+        rest = -outside[q]
+        for part in range(3):
+            piece = rest.astype(bf16).astype(f32)
+            start = jnp.where(row == 3 * QUAD + part, piece, start)
+            rest = rest - piece
+        taste_ref[q, LANES : LANES + NESTS, :] = across(start).astype(bf16)
 
     def weights(inner):
-        power = [jnp.exp2(x * lax.log2(y)) for x, y in zip(less, inner)]
+        power = [jnp.exp2(x * jnp.log(y)) for x, y in zip(less, inner)]
         total = jnp.sum(power[0] * inner[0] + power[1] * inner[1], axis=0, keepdims=True)
         total = (1.0 + total) * DRAWS
         return [x / total for x in power]
 
-    def first_half(q, b, inner, value, mu):
+    def exps(q, b, inner, power):
         o = PLACES[b][0]
-        e = jnp.exp2(mu + across(value))
-        e_ref[q, b] = e
+        e = jnp.exp2(power)
+        held[q, b] = e
         inner[o] = inner[o] + e
 
-    def second_half(q, b, weight):
-        o = PLACES[b][0]
-        p = e_ref[q, b] * weight[o]
+    def collect(b, tiles, copies):
+        o, t = PLACES[b]
+        tiles[o] = jnp.where(narrow == t, copies, tiles[o])
+
+    def sums(q, b, weight, share):
+        p = held[q, b] * weight[PLACES[b][0]]
         p = (p[:, :128] + p[:, 128:256]) + (p[:, 256:384] + p[:, 384:])
-        share = jnp.broadcast_to(jnp.sum(p, axis=1, keepdims=True), (HALF, LANES))
-        value = v_ref[q, b] + gain[o] * (t_ref[q, b] - lax.log2(jnp.maximum(share, TINY)))
-        return value, share
+        collect(b, share, jnp.broadcast_to(jnp.sum(p, axis=1, keepdims=True), (HALF, LANES)))
 
     zeros = jnp.zeros((HALF, DRAWS), f32)
-    weight = [None] * QUAD
-    count = len(PLACES)
-    for q in range(QUAD):
-        mu = dot(slot_ref[...], taste_ref[q])
+    held, base = {}, {}
+    blank = jnp.zeros((HALF, LANES), f32)
+    weight, target, value, share = [[None] * QUAD for _ in range(4)]
+    for q in range(QUAD):
+        mu = dot(slot_ref[:used, :], taste_ref[q])
         inner = [zeros, zeros]
-        for b, (o, _) in enumerate(PLACES):
+        for b, (o, _) in enumerate(PLACES[:count]):
             part = mu[b * HALF : (b + 1) * HALF] * to_two[o]
-            mu_ref[q, b] = part
-            goal = target[b * HALF : (b + 1) * HALF, q * LANES : (q + 1) * LANES] * LOG2E
-            t_ref[q, b] = goal
-            value = (goal - outside[q]) * inverse[o]
-            v_ref[q, b] = value
-            first_half(q, b, inner, value, part)
+            base[q, b] = part
+            exps(q, b, inner, part)
         weight[q] = weights(inner)
-
-    for _ in range(ITERS - 1):
-        old = list(weight)
-        for q in range(QUAD + 1):
-            inner = [zeros, zeros]
-            for b in range(count):
-                if q < QUAD:
-                    v_ref[q, b] = second_half(q, b, old[q])[0]
-                if q:
-                    first_half(q - 1, b, inner, v_ref[q - 1, b], mu_ref[q - 1, b])
-            if q:
-                weight[q - 1] = weights(inner)
-
-    back = [x * math.log(2.0) for x in rate]
-    for q in range(QUAD):
-        values = [jnp.zeros((HALF, LANES), f32)] * 2
-        shares = [jnp.zeros((HALF, LANES), f32)] * 2
-        for b, (o, t) in enumerate(PLACES):
-            value, share = second_half(q, b, weight[q])
-            values[o] = jnp.where(narrow == t, value, values[o])
-            shares[o] = jnp.where(narrow == t + 64, share, shares[o])
+        value[q] = [blank, blank]
+
+    tiles = [[blank, blank], [blank, blank]]
+    for b, (o, t) in enumerate(PLACES[:count]):
+        tile = tiles[t // 32]
+        tile[o] = jnp.where(narrow % 32 == t % 32, goals[b * HALF : (b + 1) * HALF], tile[o])
+    for q in range(QUAD):
+        target[q] = [
+            jnp.where(narrow < 32, pltpu.roll(x, (128 - 32 * q) % 128, 1), pltpu.roll(y, (160 - 32 * q) % 128, 1))
+            for x, y in zip(*tiles)
+        ]
+
+    lag = 2
+    for stage in range(ITERS * QUAD):
+        q = stage % QUAD
+        ahead = stage - lag if 0 <= stage - lag < (ITERS - 1) * QUAD else None
+        share[q], inner = [blank, blank], [zeros, zeros]
+        for b in range(count):
+            sums(q, b, weight[q], share[q])
+            if ahead is not None:
+                o, t = PLACES[b]
+                move = jnp.broadcast_to(value[ahead % QUAD][o][:, t : t + 1], (HALF, LANES))
+                exps(ahead % QUAD, b, inner, base[ahead % QUAD, b] + across(move))
+        if ahead is not None:
+            weight[ahead % QUAD] = weights(inner)
+        value[q] = [
+            v + g * (x - jnp.log(jnp.maximum(y, TINY))) for v, g, x, y in zip(value[q], gain, target[q], share[q])
+        ]
+
+    ranks = table_ref[NESTS + K :, :]
+    for q in range(QUAD):
+        final = jnp.zeros((NESTS, LANES), f32)
+        for o in range(2):
+            result = (target[q][o] - outside[q][:HALF]) + value[q][o] * (rate[o] * math.log(2.0))
+            result = jnp.where(table[o] >= 0.0, result, 0.0)
+            result = jnp.where(narrow < SLOTS, result, pltpu.roll(share[q][o], 64, 1))
+            for r in range(HALF):
+                one = jnp.broadcast_to(result[r : r + 1, :], (NESTS, LANES))
+                final = jnp.where(ranks == float(o * HALF + r), one, final)
         for n in range(2):
-            value = jnp.where(table[n] >= 0.0, values[n] * back[n], 0.0)
-            both = jnp.where(narrow < SLOTS, value, shares[n])
             for d in range(4):
-                out_ref[2 * d + n, q * HALF : (q + 1) * HALF, :] = both
+                out_ref[2 * d + n, q * HALF : (q + 1) * HALF, :] = final[n * HALF : (n + 1) * HALF]
+
+
+def contract(x_ref, t0_ref, t1_ref, t2_ref, t3_ref, table_ref, hot_ref, pick_ref, mask_ref, out_ref,
+             slot_ref, taste_ref, l_ref):
+    inputs = (x_ref, (t0_ref, t1_ref, t2_ref, t3_ref), table_ref, hot_ref, pick_ref, mask_ref, out_ref)
+    short = table_ref[HALF, CUT] < 0.0
+
+    @pl.when(short)
+    def _():
+        solve(SHORT, *inputs, slot_ref, taste_ref, l_ref)
+
+    @pl.when(jnp.logical_not(short))
+    def _():
+        solve(len(PLACES), *inputs, slot_ref, taste_ref, l_ref)
 
 
 def unpack(r_ref, value_ref, share_ref):
@@ -266,7 +322,7 @@
         arrange,
         name="arrange",
         out_shape=(
-            jax.ShapeDtypeStruct((NESTS + K, LANES), f32),
+            jax.ShapeDtypeStruct((NESTS + K + NESTS, LANES), f32),
             jax.ShapeDtypeStruct((rows, DRAWS), bf16),
             jax.ShapeDtypeStruct((rows, LANES), bf16),
             jax.ShapeDtypeStruct((rows, LANES), bf16),
@@ -285,8 +341,6 @@
             piece = lax.ppermute(piece, "draw", [(i, (i + shift) % 4) for i in range(4)])
         tastes.append(piece)
 
-    big = (QUAD, len(PLACES), HALF, DRAWS)
-    small = (QUAD, len(PLACES), HALF, LANES)
     results = pl.pallas_call(
         contract,
         name="contract",
@@ -294,12 +348,8 @@
         in_specs=[VMEM] * 9,
         out_specs=VMEM,
         scratch_shapes=[
-            pltpu.VMEM((rows, LANES), bf16),
-            pltpu.VMEM((QUAD, QUAD * K, DRAWS), bf16),
-            pltpu.VMEM(big, f32),
-            pltpu.VMEM(big, f32),
-            pltpu.VMEM(small, f32),
-            pltpu.VMEM(small, f32),
+            pltpu.VMEM((rows, 2 * LANES), bf16),
+            pltpu.VMEM((QUAD, 2 * LANES, DRAWS), bf16),
             pltpu.VMEM((BLOCKS * 8, LANES), f32),
         ],
         compiler_params=pltpu.CompilerParams(vmem_limit_bytes=36 * MIB),

time: 45.1 us -> 43.9 us (0.973)
  Pallas kernels: 9.62 us -> 8.65 us
    pallas_call x1, Pallas kernels: 5.83 us -> 4.59 us  [shards(): pl.pallas_call(contract, name='contract', out_shape=jax.ShapeDtypeStruct(...]
where the time goes in v4:
time: 43.9 us; the launch traced here: 43.6 us
  starting transfers between devices  17.7 us (40%)
  blocking collectives  13.2 us (30%)
  Pallas kernels  8.65 us (20%)
  waiting for transfers between devices  3 us (7%)
  between operations  0.79 us (2%)
    all_to_all x1, blocking collectives, shards(): lax.all_to_all(results, ('draw', 'nest'), split_axis=0, concat_axis=0, ti...  13.2 us
    all_to_all x1, starting transfers between devices, shards(): recv = lax.all_to_all(send, 'mkt', split_axis=0, concat_axis=0, tiled=True)  10.2 us
    ppermute x3, starting transfers between devices, shards(): lax.ppermute(piece, 'draw', [(i, (i + shift) % 4) for i in range(4)])  5.3 us
    pallas_call x1, Pallas kernels, shards(): pl.pallas_call(contract, name='contract', out_shape=jax.ShapeDtypeStruct(...  4.59 us
    ppermute x1, waiting for transfers between devices, shards(): far = lax.ppermute(near, 'nest', [(0, 1), (1, 0)])  2.99 us
    pallas_call x1, Pallas kernels, shards(): pl.pallas_call(pack, name='pack', out_shape=jax.ShapeDtypeStruct((BLOCKS,...  2.71 us
    ppermute x1, starting transfers between devices, shards(): far = lax.ppermute(near, 'nest', [(0, 1), (1, 0)])  2.15 us
  transfers between devices with their start and end apart: 5, of which 1 were waited for; matrix products, arithmetic and copies ran while one was open for 1% of the time, Pallas kernels for 1%

profile of v4, /device:TPU:2, one launch (start us, length us, event | category | flops | bytes accessed | tf_op | source)
XLA Modules:
  0.0 43.6 jit_solution(5572402092882659868)
XLA Ops:
  0.6 2.7 %pack.1 = bf16[32,24,128]{2,1,0:T(8,128)(2,1)} custom-call(bf16[32,16,1024]{2,1,0:T(8,128)(2,1)} %f_hbm.1, f32[16,1024]{1,0:T(8,128)} %l_hbm.1), custom_call_target="tpu_custom_call" | custom-call | tf_op jit(solution)/shard_map/pack/pallas_call | solution.py:298
  3.3 0.0 copy-start.1
  3.4 10.2 %all-to-all-start = ((bf16[32,24,128]{2,1,0:T(8,128)(2,1)}), bf16[32,24,128]{2,1,0:T(8,128)(2,1)S(1)}, u32[]{:S(2)}, u32[]{:S(2)}) async-start(bf16[32,24,128]{2,1,0:T(8,128)(2,1)} %pack.1), calls=%async_computation | async-start | bytes 393216 | tf_op jit(solution)/shard_map/all_to_all | solution.py:314
  13.7 0.0 copy-done.1
  13.7 0.0 copy-start.3
  13.7 3.1 %collective-permute-start.2 = (bf16[4,32,128]{2,1,0:T(8,128)(2,1)S(1)}, bf16[4,32,128]{2,1,0:T(8,128)(2,1)S(1)}, u32[]{:S(2)}, u32[]{:S(2)}) collective-permute-start(bf16[4,32,128]{2,1,0:T(8,128)(2,1)S(1)} %get-tuple-element.10), channel_id=1, source_target_pairs={{0,6},{2,0},{4,2},{6,4},{1,7},{3,1},{5,3},{7,5},{8,14},{10,8},{12,... | collective-permute-start | bytes 98312 | tf_op jit(solution)/shard_map/ppermute | solution.py:341
  16.8 0.0 copy-start.2
  16.8 0.0 collective-permute-start
  16.8 2.2 %collective-permute-start.1 = (bf16[4,32,128]{2,1,0:T(8,128)(2,1)S(1)}, bf16[4,32,128]{2,1,0:T(8,128)(2,1)S(1)}, u32[]{:S(2)}, u32[]{:S(2)}) collective-permute-start(bf16[4,32,128]{2,1,0:T(8,128)(2,1)S(1)} %get-tuple-element.13), channel_id=1, source_target_pairs={{0,4},{2,6},{4,0},{6,2},{1,5},{3,7},{5,1},{7,3},{8,12},{10,14},{12... | collective-permute-start | bytes 98312 | tf_op jit(solution)/shard_map/ppermute | solution.py:341
  19.0 0.0 copy-done.3
  19.0 0.1 copy.8
  19.1 0.0 copy-done.2
  19.1 0.1 pad.2.clone
  19.2 0.1 maximum_maximum_fusion.near_ref
  19.3 0.0 copy-start
  19.3 2.1 %collective-permute-start.3 = (f32[8,128]{1,0:T(8,128)S(1)}, f32[8,128]{1,0:T(8,128)S(1)}, u32[]{:S(2)}, u32[]{:S(2)}) collective-permute-start(f32[8,128]{1,0:T(8,128)S(1)} %maximum_maximum_fusion.near_ref), channel_id=1, source_target_pairs={{0,1},{1,0},{2,3},{3,2},{4,5},{5,4},{6,7},{7,6},{8,9},{9,8},{10,11... | collective-permute-start | bytes 12296 | tf_op jit(solution)/shard_map/ppermute | solution.py:319
  21.4 3.0 %collective-permute-done.3.far_ref = f32[8,128]{1,0:T(8,128)S(1)} collective-permute-done((f32[8,128]{1,0:T(8,128)S(1)}, f32[8,128]{1,0:T(8,128)S(1)}, u32[]{:S(2)}, u32[]{:S(2)}) %collective-permute-start.3) | collective-permute-done | bytes 4128 | tf_op jit(solution)/shard_map/ppermute | solution.py:319
  24.4 0.0 copy-done
  24.4 0.6 %arrange.1 = (f32[64,128]{1,0:T(8,128)S(1)}, bf16[768,512]{1,0:T(8,128)(2,1)S(1)}, bf16[768,128]{1,0:T(8,128)(2,1)S(1)}, bf16[768,128]{1,0:T(8,128)(2,1)S(1)}) custom-call(f32[8,128]{1,0:T(8,128)S(1)} %maximum_maximum_fusion.near_ref, f32[8,128]{1,0:T(8,128)S(1)} %collective-permute-done.3.far_ref, f32[1,32]{1,0:T(1,128)S(1)} %bitcast.4), custom_call_target="tpu_custom_call" | custom-call | flops 2000000 | bytes 2000000 | tf_op jit(solution)/shard_map/arrange/pallas_call | solution.py:321
  25.0 0.0 collective-permute-done.2.t3_ref
  25.0 0.0 collective-permute-done.t1_ref
  25.0 0.0 collective-permute-done.1.t2_ref
  25.0 0.0 all-to-all-done.x_ref
  25.0 4.6 %contract.1 = f32[8,32,128]{2,1,0:T(8,128)S(1)} custom-call(bf16[32,24,128]{2,1,0:T(8,128)(2,1)S(1)} %all-to-all-done.x_ref, bf16[4,32,128]{2,1,0:T(8,128)(2,1)S(1)} %get-tuple-element.12.t0_ref, bf16[4,32,128]{2,1,0:T(8,128)(2,1)S(1)} %collective-permute-done.t1_ref, bf16[4,32,128]{2,1,0:T(8,128)(2,1)S(1)} %collective-permute-done.1.t2_ref, ...), custom_call_target="tpu_custom_call" | custom-call | tf_op jit(solution)/shard_map/contract/pallas_call | solution.py:344
  29.6 13.2 %all_to_all.10 = f32[8,32,128]{2,1,0:T(8,128)S(1)} all-to-all(f32[8,32,128]{2,1,0:T(8,128)S(1)} %contract.1), channel_id=1, replica_groups=mesh['mkt'=32,'draw'=4,'nest'=2] {'draw','nest'}, dimensions={0} | all-to-all | bytes 262144 | tf_op jit(solution)/shard_map/all_to_all | solution.py:357
  42.9 0.8 %unpack.1 = (f32[32,384]{1,0:T(8,128)}, f32[32,384]{1,0:T(8,128)}) custom-call(f32[256,128]{1,0:T(8,128)S(1)} %bitcast.3), custom_call_target="tpu_custom_call" | custom-call | tf_op jit(solution)/shard_map/unpack/pallas_call | solution.py:359
  (3 shorter events, 0.0 us)
Async XLA Ops:
  3.3 10.3 %copy-start.1 = (bf16[32,32,128]{2,1,0:T(8,128)(2,1)S(1)}, bf16[32,32,128]{2,1,0:T(8,128)(2,1)}, u32[]{:S(2)}) copy-start(bf16[32,32,128]{2,1,0:T(8,128)(2,1)} %param.7) | copy-start | bytes 786436
  3.4 21.7 %all-to-all-start = ((bf16[32,24,128]{2,1,0:T(8,128)(2,1)}), bf16[32,24,128]{2,1,0:T(8,128)(2,1)S(1)}, u32[]{:S(2)}, u32[]{:S(2)}) async-start(bf16[32,24,128]{2,1,0:T(8,128)(2,1)} %pack.1), calls=%async_computation | async-start | bytes 393216 | tf_op jit(solution)/shard_map/all_to_all | solution.py:314
  13.7 5.3 %copy-start.3 = (f32[8]{0:T(128)S(1)}, f32[8]{0:T(128)}, u32[]{:S(2)}) copy-start(f32[8]{0:T(128)} %param.9) | copy-start | bytes 100
  13.7 11.3 %collective-permute-start.2 = (bf16[4,32,128]{2,1,0:T(8,128)(2,1)S(1)}, bf16[4,32,128]{2,1,0:T(8,128)(2,1)S(1)}, u32[]{:S(2)}, u32[]{:S(2)}) collective-permute-start(bf16[4,32,128]{2,1,0:T(8,128)(2,1)S(1)} %get-tuple-element.10), channel_id=1, source_target_pairs={{0,6},{2,0},{4,2},{6,4},{1,7},{3,1},{5,3},{7,5},{8,14},{10,8},{12,... | collective-permute-start | bytes 98312 | tf_op jit(solution)/shard_map/ppermute | solution.py:341
  16.8 2.3 %copy-start.2 = (s32[8,48]{1,0:T(8,128)S(1)}, s32[8,48]{1,0:T(8,128)}, u32[]{:S(2)}) copy-start(s32[8,48]{1,0:T(8,128)} %param.10) | copy-start | bytes 4612
  16.8 8.2 %collective-permute-start = (bf16[4,32,128]{2,1,0:T(8,128)(2,1)S(1)}, bf16[4,32,128]{2,1,0:T(8,128)(2,1)S(1)}, u32[]{:S(2)}, u32[]{:S(2)}) collective-permute-start(bf16[4,32,128]{2,1,0:T(8,128)(2,1)S(1)} %get-tuple-element.11), channel_id=1, source_target_pairs={{0,2},{2,4},{4,6},{6,0},{1,3},{3,5},{5,7},{7,1},{8,10},{10,12},{12... | collective-permute-start | bytes 98312 | tf_op jit(solution)/shard_map/ppermute | solution.py:341
  16.8 8.2 %collective-permute-start.1 = (bf16[4,32,128]{2,1,0:T(8,128)(2,1)S(1)}, bf16[4,32,128]{2,1,0:T(8,128)(2,1)S(1)}, u32[]{:S(2)}, u32[]{:S(2)}) collective-permute-start(bf16[4,32,128]{2,1,0:T(8,128)(2,1)S(1)} %get-tuple-element.13), channel_id=1, source_target_pairs={{0,4},{2,6},{4,0},{6,2},{1,5},{3,7},{5,1},{7,3},{8,12},{10,14},{12... | collective-permute-start | bytes 98312 | tf_op jit(solution)/shard_map/ppermute | solution.py:341
  19.3 5.1 %copy-start = (f32[32]{0:T(128)S(1)}, f32[32]{0:T(128)}, u32[]{:S(2)}) copy-start(f32[32]{0:T(128)} %param.8) | copy-start | bytes 388
  19.3 5.1 %collective-permute-start.3 = (f32[8,128]{1,0:T(8,128)S(1)}, f32[8,128]{1,0:T(8,128)S(1)}, u32[]{:S(2)}, u32[]{:S(2)}) collective-permute-start(f32[8,128]{1,0:T(8,128)S(1)} %maximum_maximum_fusion.near_ref), channel_id=1, source_target_pairs={{0,1},{1,0},{2,3},{3,2},{4,5},{5,4},{6,7},{7,6},{8,9},{9,8},{10,11... | collective-permute-start | bytes 12296 | tf_op jit(solution)/shard_map/ppermute | solution.py:319

commit v5 on v4

--- a/solution.py
+++ b/solution.py
@@ -19,7 +19,7 @@
 DRAWS = 512
 MARKETS = 1024
 LANES = 128
-ROWS = 24
+ROWS = 18
 LOG2E = 1.0 / math.log(2.0)
 LOW = -1e30
 MIB = 1024 * 1024
@@ -46,7 +46,7 @@
     return lax.dot_general(a, b, (((1,), (1,)), ((), ())), preferred_element_type=f32)
 
 
-def pack(f_hbm, l_hbm, out_hbm, f_ref, l_ref, g_ref, o_ref, s_ref, out_ref, sems):
+def pack(f_hbm, l_hbm, out_hbm, f_ref, l_ref, g_ref, o_ref, out_ref, sems):
     loads = [pltpu.make_async_copy(l_hbm, l_ref, sems.at[PARTS])]
     for c in range(PARTS):
         part = pl.ds(c * K // PARTS, K // PARTS)
@@ -69,9 +69,8 @@
     own = (iota((LANES, LANES), 0) // PROD) % QUAD == iota((LANES, LANES), 1) // BLOCKS
     first = jnp.concatenate([logs[:PROD]] * QUAD + [logs[PROD : 2 * PROD]] * QUAD, axis=0)
     second = jnp.concatenate([logs[2 * PROD :]] * QUAD + [jnp.zeros((64, LANES), f32)], axis=0)
-    s_ref[...] = jnp.zeros_like(s_ref)
-    s_ref[pl.ds(0, BLOCKS, stride=8), :] = dot_t(spread, jnp.where(own, first, 0.0).astype(bf16))
-    s_ref[pl.ds(1, BLOCKS, stride=8), :] = dot_t(spread, jnp.where(own, second, 0.0).astype(bf16))
+    o_ref[pl.ds(PROD, BLOCKS, stride=ROWS), :] = dot_t(spread, jnp.where(own, first, 0.0).astype(bf16))
+    o_ref[pl.ds(PROD + 1, BLOCKS, stride=ROWS), :] = dot_t(spread, jnp.where(own, second, 0.0).astype(bf16))
 
     rows = K * PROD // PARTS
     for c in range(PARTS):
@@ -85,16 +84,13 @@
         parts.append(jnp.where(own, jnp.concatenate([part] * QUAD, axis=0), 0.0).astype(bf16))
     goods = dot_t(spread, jnp.concatenate(parts, axis=0))
     for j in range(PROD):
-        o_ref[pl.ds(j, BLOCKS, stride=PROD), :] = goods[:, j * LANES : (j + 1) * LANES]
+        o_ref[pl.ds(j, BLOCKS, stride=ROWS), :] = goods[:, j * LANES : (j + 1) * LANES]
     stores = []
+    half = BLOCKS * ROWS // 2
     for c in range(2):
-        half = slice(c * BLOCKS // 2, (c + 1) * BLOCKS // 2)
-        goods = o_ref[c * 256 : (c + 1) * 256, :].reshape(BLOCKS // 2, PROD, LANES)
-        out_ref[half, :PROD, :] = goods.astype(bf16)
-        logs = s_ref[c * 128 : (c + 1) * 128, :].reshape(BLOCKS // 2, 8, LANES)
-        out_ref[half, PROD:, :] = logs.astype(bf16)
-        half = pl.ds(c * BLOCKS // 2, BLOCKS // 2)
-        stores.append(pltpu.make_async_copy(out_ref.at[half], out_hbm.at[half], sems.at[c]))
+        out_ref[c * half : (c + 1) * half, :] = o_ref[c * half : (c + 1) * half, :].astype(bf16)
+        part = pl.ds(c * half, half)
+        stores.append(pltpu.make_async_copy(out_ref.at[part], out_hbm.at[part], sems.at[c]))
         stores[-1].start()
     for store in stores:
         store.wait()
@@ -104,9 +100,9 @@
     return jnp.concatenate([x] * (DRAWS // LANES), axis=1)
 
 
-def arrange(near_ref, far_ref, scale_ref, table_ref, hot_ref, pick_ref, mask_ref):
-    near, far = near_ref[...], far_ref[...]
+def arrange(near_ref, next_ref, scale_ref, table_ref, hot_ref, pick_ref, mask_ref):
     first = lax.axis_index("nest") == 0
+    near, far = near_ref[...], next_ref[QUAD * K :, :]
     table = jnp.concatenate([jnp.where(first, near, far), jnp.where(first, far, near)], axis=0)
     row, lane = iota((NESTS, LANES), 0), iota((NESTS, LANES), 1)
     filled = jnp.where((lane < SLOTS) & (table >= 0.0), 1.0, 0.0)
@@ -153,9 +149,9 @@
     less = [across((x - 1.0) * LOG2E) for x in rate]
     narrow = iota((HALF, LANES), 1)
 
-    l_ref[...] = x_ref[:, PROD:, :].astype(f32).reshape(BLOCKS * 8, LANES)
-    top = l_ref[pl.ds(0, BLOCKS, stride=8), :]
-    rest = l_ref[pl.ds(1, BLOCKS, stride=8), :]
+    l_ref[...] = x_ref[...].astype(f32)
+    top = l_ref[pl.ds(PROD, BLOCKS, stride=ROWS), :]
+    rest = l_ref[pl.ds(PROD + 1, BLOCKS, stride=ROWS), :]
     both = jnp.concatenate([top, rest], axis=1)
     lane = iota((BLOCKS, 2 * LANES), 1)
     lows = (iota((BLOCKS, 2 * LANES), 0) == 0) & (lane < 64) & (lane % PROD == PROD - 1)
@@ -163,13 +159,13 @@
     rows = dot(pick_ref[:used, :], both).astype(bf16)
     mask = mask_ref[:used, :]
     rows = rows * jnp.concatenate([mask, mask], axis=1)
-    source, lane = iota((2 * LANES, LANES), 0), iota((2 * LANES, LANES), 1)
-    fold = jnp.where((source // 64) * QUAD + (source // PROD) % QUAD == lane, 1.0, 0.0).astype(bf16)
-    parts = dot(rows, fold)
+    source, lane = iota((2 * LANES, 2 * LANES), 0), iota((2 * LANES, 2 * LANES), 1)
+    market = (source // PROD) % QUAD
+    fold = ((lane < LANES) & ((source // 64) * QUAD + market == lane)) | ((lane >= LANES) & (market == lane // 32 - QUAD))
+    folded = dot(rows, jnp.where(fold, 1.0, 0.0).astype(bf16))
+    goals = folded[:, LANES:]
     ones = jnp.where((narrow >= 3 * QUAD) & (narrow < 3 * QUAD + 3), 1.0, 0.0)
-    slot_ref[:used, LANES:] = (parts + jnp.concatenate([ones] * count, axis=0)).astype(bf16)
-    copies = jnp.where((source // PROD) % QUAD == lane // 32, 1.0, 0.0).astype(bf16)
-    goals = dot(rows, copies)
+    slot_ref[:used, LANES:] = (folded[:, :LANES] + jnp.concatenate([ones] * count, axis=0)).astype(bf16)
     whole = (top + pltpu.roll(top, 64, 1)) + rest
     shares = jnp.exp(whole)
     column = iota((BLOCKS, LANES), 1)
@@ -179,13 +175,14 @@
         total = 1.0 - jnp.sum(jnp.sum(inside, axis=1, keepdims=True), axis=0, keepdims=True)
         outside.append(jnp.log(jnp.broadcast_to(total, (NESTS, LANES))))
 
-    x = x_ref[:, :PROD, :].reshape(BLOCKS * PROD, LANES)
+    x = jnp.concatenate([l_ref[i * ROWS : i * ROWS + PROD, :] for i in range(BLOCKS)], axis=0).astype(bf16)
     slot_ref[:used, :LANES] = dot(hot_ref[:used, :], x).astype(bf16)
     scale = table_ref[NESTS : NESTS + K, :]
     taste_ref[...] = jnp.zeros_like(taste_ref)
     for q in range(QUAD):
         for b, ref in enumerate(taste_refs):
-            taste = (scale * ref[q].astype(f32)).astype(bf16)
+            taste = ref[q] if b != 1 else ref[q * K : (q + 1) * K, :]
+            taste = (scale * taste.astype(f32)).astype(bf16)
             taste_ref[q, q * K : (q + 1) * K, b * LANES : (b + 1) * LANES] = taste
         row = iota((NESTS, LANES), 0)
         start = jnp.where((row < 3 * QUAD) & (row % QUAD == q), 1.0, 0.0)
@@ -298,25 +295,36 @@
     send = pl.pallas_call(
         pack,
         name="pack",
-        out_shape=jax.ShapeDtypeStruct((BLOCKS, ROWS, LANES), bf16),
+        out_shape=jax.ShapeDtypeStruct((BLOCKS * ROWS, LANES), bf16),
         in_specs=[HBM, HBM],
         out_specs=HBM,
         scratch_shapes=[
             pltpu.VMEM((K, PROD, MARKETS), bf16),
             pltpu.VMEM((PROD, MARKETS), f32),
             pltpu.VMEM((K * PROD, LANES), f32),
-            pltpu.VMEM((BLOCKS * PROD, LANES), f32),
-            pltpu.VMEM((BLOCKS * 8, LANES), f32),
-            pltpu.VMEM((BLOCKS, ROWS, LANES), bf16),
+            pltpu.VMEM((BLOCKS * ROWS, LANES), f32),
+            pltpu.VMEM((BLOCKS * ROWS, LANES), bf16),
             pltpu.SemaphoreType.DMA((PARTS + 1,)),
         ],
     )(features, log_share)
+    send = send.reshape(BLOCKS, ROWS // 2, 2, LANES)
     recv = lax.all_to_all(send, "mkt", split_axis=0, concat_axis=0, tiled=True)
+    recv = recv.reshape(BLOCKS * ROWS, LANES)
+
+    d, n = lax.axis_index("draw"), lax.axis_index("nest")
+
+    def tastes(shift, nest):
+        return lax.dynamic_slice_in_dim(taste_draws, (d + shift) % 4 * 8 + nest * QUAD, QUAD, 0)
 
     near = jnp.concatenate(
         [members.astype(f32), nest_param[:, None], jnp.zeros((HALF, LANES - SLOTS - 1), f32)], axis=1
     )
-    far = lax.ppermute(near, "nest", [(0, 1), (1, 0)])
+    both = jnp.concatenate([tastes(1, 1 - n).astype(f32).reshape(QUAD * K, LANES), near], axis=0)
+    ring = [(2 * i + j, (i + 1) % 4 * 2 + 1 - j) for i in range(4) for j in range(2)]
+    both = lax.ppermute(both, ("draw", "nest"), ring)
+    others = []
+    for shift in (2, 3):
+        others.append(lax.ppermute(tastes(shift, n), "draw", [(i, (i + shift) % 4) for i in range(4)]))
     rows = len(PLACES) * HALF
     plan = pl.pallas_call(
         arrange,
@@ -331,16 +339,7 @@
         out_specs=(VMEM,) * 4,
         cost_estimate=pl.CostEstimate(flops=2_000_000, bytes_accessed=2_000_000, transcendentals=0),
         compiler_params=pltpu.CompilerParams(vmem_limit_bytes=4 * MIB),
-    )(near, far, taste_scale.reshape(1, K))
-    d, n = lax.axis_index("draw"), lax.axis_index("nest")
-    tastes = []
-    for shift in range(4):
-        to = (d + shift) % 4
-        piece = lax.dynamic_slice_in_dim(taste_draws, to * 8 + n * QUAD, QUAD, 0)
-        if shift:
-            piece = lax.ppermute(piece, "draw", [(i, (i + shift) % 4) for i in range(4)])
-        tastes.append(piece)
-
+    )(near, both, taste_scale.reshape(1, K))
     results = pl.pallas_call(
         contract,
         name="contract",
@@ -350,10 +349,10 @@
         scratch_shapes=[
             pltpu.VMEM((rows, 2 * LANES), bf16),
             pltpu.VMEM((QUAD, 2 * LANES, DRAWS), bf16),
-            pltpu.VMEM((BLOCKS * 8, LANES), f32),
+            pltpu.VMEM((BLOCKS * ROWS, LANES), f32),
         ],
         compiler_params=pltpu.CompilerParams(vmem_limit_bytes=36 * MIB),
-    )(recv, *tastes, *plan)
+    )(recv, tastes(0, n), both, *others, *plan)
     gathered = lax.all_to_all(results, ("draw", "nest"), split_axis=0, concat_axis=0, tiled=True)
     shape = jax.ShapeDtypeStruct((32, HALF * SLOTS), f32)
     return pl.pallas_call(

time: 43.9 us -> 46.9 us (1.068)
  waiting for transfers between devices: 3 us -> 5.75 us
  local copies, waits for them, and re-layouts: 0.2 us -> 1.54 us
  starting transfers between devices: 17.7 us -> 16.4 us
    ppermute x4 -> x3, waiting for transfers between devices: 3 us -> 5.75 us  [the longest x1 5.75 us: shards(): both = lax.ppermute(both, ('draw', 'nest'), ring)]
    ppermute x4 -> x3, starting transfers between devices: 7.45 us -> 6.27 us  [the longest x2 3.72 us: shards(): lax.ppermute(tastes(shift, n), 'draw', [(i, (i + shift) % 4) for i in ran...]
    dynamic_slice x1, local copies, waits for them, and re-layouts: 0.02 us -> 0.83 us  [tastes(): lax.dynamic_slice_in_dim(taste_draws, (d + shift) % 4 * 8 + nest * QUAD,...]
    unnamed x8 -> x6, local copies, waits for them, and re-layouts: 0.02 us -> 0.63 us
  transfers between devices with their start and end apart: 5 -> 4, of which waited for: 1 -> 1; matrix products, arithmetic and copies ran while one was open for 1% -> 1% of each run, Pallas kernels for 1% -> 7%
where the time goes in v5:
time: 46.9 us; the launch traced here: 46.5 us
  starting transfers between devices  16.4 us (35%)
  blocking collectives  13.5 us (29%)
  Pallas kernels  8.42 us (18%)
  waiting for transfers between devices  5.75 us (12%)
  local copies, waits for them, and re-layouts  1.54 us (3%)
  between operations  0.78 us (2%)
    all_to_all x1, blocking collectives, shards(): lax.all_to_all(results, ('draw', 'nest'), split_axis=0, concat_axis=0, ti...  13.5 us
    all_to_all x1, starting transfers between devices, shards(): recv = lax.all_to_all(send, 'mkt', split_axis=0, concat_axis=0, tiled=True)  10.1 us
    ppermute x1, waiting for transfers between devices, shards(): both = lax.ppermute(both, ('draw', 'nest'), ring)  5.75 us
    pallas_call x1, Pallas kernels, shards(): pl.pallas_call(contract, name='contract', out_shape=jax.ShapeDtypeStruct(...  4.41 us
    ppermute x2, starting transfers between devices, shards(): lax.ppermute(tastes(shift, n), 'draw', [(i, (i + shift) % 4) for i in ran...  3.72 us
    pallas_call x1, Pallas kernels, shards(): pl.pallas_call(pack, name='pack', out_shape=jax.ShapeDtypeStruct((BLOCKS...  2.67 us
    ppermute x1, starting transfers between devices, shards(): both = lax.ppermute(both, ('draw', 'nest'), ring)  2.55 us
  transfers between devices with their start and end apart: 4, of which 1 were waited for; matrix products, arithmetic and copies ran while one was open for 1% of the time, Pallas kernels for 7%

profile of v5, /device:TPU:2, one launch (start us, length us, event | category | flops | bytes accessed | tf_op | source)
XLA Modules:
  0.0 46.5 jit_solution(8782443308360546730)
XLA Ops:
  0.7 0.8 %constant_dynamic-slice_fusion = (bf16[4,32,128]{2,1,0:T(8,128)(2,1)S(1)}, bf16[4,32,128]{2,1,0:T(8,128)(2,1)S(1)}, bf16[4,32,128]{2,1,0:T(8,128)(2,1)S(1)}, bf16[4,32,128]{2,1,0:T(8,128)(2,1)S(1)}) fusion(bf16[32,32,128]{2,1,0:T(8,128)(2,1)} %param.7, s32[]{:T(128)S(6)} %select_n.38, s32[]{:T(128)S(6)} %select_n.34, s32[]{:T(128)S(6)} %select_n.32, ...), kind=kLoop, calls=%fused_computation.3 | loop fusion | bytes 262160 | tf_op jit(solution)/shard_map/dynamic_slice | solution.py:317
  1.5 3.1 %collective-permute-start.2 = (bf16[4,32,128]{2,1,0:T(8,128)(2,1)S(1)}, bf16[4,32,128]{2,1,0:T(8,128)(2,1)S(1)}, u32[]{:S(2)}, u32[]{:S(2)}) collective-permute-start(bf16[4,32,128]{2,1,0:T(8,128)(2,1)S(1)} %get-tuple-element.10), channel_id=1, source_target_pairs={{0,6},{2,0},{4,2},{6,4},{1,7},{3,1},{5,3},{7,5},{8,14},{10,8},{12,... | collective-permute-start | bytes 98312 | tf_op jit(solution)/shard_map/ppermute | solution.py:327
  4.6 0.6 %collective-permute-start.1 = (bf16[4,32,128]{2,1,0:T(8,128)(2,1)S(1)}, bf16[4,32,128]{2,1,0:T(8,128)(2,1)S(1)}, u32[]{:S(2)}, u32[]{:S(2)}) collective-permute-start(bf16[4,32,128]{2,1,0:T(8,128)(2,1)S(1)} %get-tuple-element.13), channel_id=1, source_target_pairs={{0,4},{2,6},{4,0},{6,2},{1,5},{3,7},{5,1},{7,3},{8,12},{10,14},{12... | collective-permute-start | bytes 98312 | tf_op jit(solution)/shard_map/ppermute | solution.py:327
  5.2 2.7 %pack.1 = bf16[576,128]{1,0:T(8,128)(2,1)} custom-call(bf16[32,16,1024]{2,1,0:T(8,128)(2,1)} %f_hbm.1, f32[16,1024]{1,0:T(8,128)} %l_hbm.1), custom_call_target="tpu_custom_call" | custom-call | tf_op jit(solution)/shard_map/pack/pallas_call | solution.py:295
  7.9 10.1 %all-to-all-start = ((bf16[32,9,2,128]{3,2,1,0:T(2,128)(2,1)}), bf16[32,9,2,128]{3,2,1,0:T(2,128)(2,1)S(1)}, u32[]{:S(2)}, u32[]{:S(2)}) async-start(bf16[32,9,2,128]{3,2,1,0:T(2,128)(2,1)} %bitcast.11), calls=%async_computation | async-start | bytes 294912 | tf_op jit(solution)/shard_map/all_to_all | solution.py:311
  18.0 0.0 copy-start.2
  18.1 0.0 copy-start.1
  18.1 0.6 %copy-done.2 = f32[8]{0:T(128)S(1)} copy-done((f32[8]{0:T(128)S(1)}, f32[8]{0:T(128)}, u32[]{:S(2)}) %copy-start.2) | copy-done | bytes 56
  18.7 0.1 copy.8
  18.8 0.0 copy-done.1
  18.8 0.1 maximum_maximum_fusion
  18.8 2.5 %collective-permute-start = (f32[136,128]{1,0:T(8,128)S(1)}, f32[136,128]{1,0:T(8,128)S(1)}, u32[]{:S(2)}, u32[]{:S(2)}) collective-permute-start(f32[136,128]{1,0:T(8,128)S(1)} %maximum_maximum_fusion), channel_id=1, source_target_pairs={{0,3},{1,2},{2,5},{3,4},{4,7},{5,6},{6,1},{7,0},{8,11},{9,10},{10,... | collective-permute-start | bytes 208904 | tf_op jit(solution)/shard_map/ppermute | solution.py:324
  21.4 0.1 pad_maximum_fusion.near_ref
  21.5 0.0 copy-start
  21.5 5.7 %collective-permute-done.next_ref.t1_ref = f32[136,128]{1,0:T(8,128)S(1)} collective-permute-done((f32[136,128]{1,0:T(8,128)S(1)}, f32[136,128]{1,0:T(8,128)S(1)}, u32[]{:S(2)}, u32[]{:S(2)}) %collective-permute-start) | collective-permute-done | bytes 69664 | tf_op jit(solution)/shard_map/ppermute | solution.py:324
  27.2 0.0 copy-done
  27.2 0.6 %arrange.1 = (f32[64,128]{1,0:T(8,128)S(1)}, bf16[768,512]{1,0:T(8,128)(2,1)S(1)}, bf16[768,128]{1,0:T(8,128)(2,1)S(1)}, bf16[768,128]{1,0:T(8,128)(2,1)S(1)}) custom-call(f32[8,128]{1,0:T(8,128)S(1)} %pad_maximum_fusion.near_ref, f32[136,128]{1,0:T(8,128)S(1)} %collective-permute-done.next_ref.t1_ref, f32[1,32]{1,0:T(1,128)S(1)} %bitcast.10), custom_call_target="tpu_custom_call" | custom-call | flops 2000000 | bytes 2000000 | tf_op jit(solution)/shard_map/arrange/pallas_call | solution.py:329
  27.8 0.0 collective-permute-done.2.t3_ref
  27.8 0.0 collective-permute-done.1.t2_ref
  27.8 0.0 all-to-all-done
  27.8 4.4 %contract.1 = f32[8,32,128]{2,1,0:T(8,128)S(1)} custom-call(bf16[576,128]{1,0:T(8,128)(2,1)S(1)} %bitcast.8, bf16[4,32,128]{2,1,0:T(8,128)(2,1)S(1)} %get-tuple-element.12.t0_ref, f32[136,128]{1,0:T(8,128)S(1)} %collective-permute-done.next_ref.t1_ref, bf16[4,32,128]{2,1,0:T(8,128)(2,1)S(1)} %collective-permute-done.1.t2_ref, ...), custom_call_target="tpu_custom_call" | custom-call | tf_op jit(solution)/shard_map/contract/pallas_call | solution.py:343
  32.3 13.5 %all_to_all.10 = f32[8,32,128]{2,1,0:T(8,128)S(1)} all-to-all(f32[8,32,128]{2,1,0:T(8,128)S(1)} %contract.1), channel_id=1, replica_groups=mesh['mkt'=32,'draw'=4,'nest'=2] {'draw','nest'}, dimensions={0} | all-to-all | bytes 262144 | tf_op jit(solution)/shard_map/all_to_all | solution.py:356
  45.8 0.8 %unpack.1 = (f32[32,384]{1,0:T(8,128)}, f32[32,384]{1,0:T(8,128)}) custom-call(f32[256,128]{1,0:T(8,128)S(1)} %bitcast.9), custom_call_target="tpu_custom_call" | custom-call | tf_op jit(solution)/shard_map/unpack/pallas_call | solution.py:358
  (3 shorter events, 0.0 us)
Async XLA Ops:
  1.5 26.3 %collective-permute-start.2 = (bf16[4,32,128]{2,1,0:T(8,128)(2,1)S(1)}, bf16[4,32,128]{2,1,0:T(8,128)(2,1)S(1)}, u32[]{:S(2)}, u32[]{:S(2)}) collective-permute-start(bf16[4,32,128]{2,1,0:T(8,128)(2,1)S(1)} %get-tuple-element.10), channel_id=1, source_target_pairs={{0,6},{2,0},{4,2},{6,4},{1,7},{3,1},{5,3},{7,5},{8,14},{10,8},{12,... | collective-permute-start | bytes 98312 | tf_op jit(solution)/shard_map/ppermute | solution.py:327
  4.6 23.2 %collective-permute-start.1 = (bf16[4,32,128]{2,1,0:T(8,128)(2,1)S(1)}, bf16[4,32,128]{2,1,0:T(8,128)(2,1)S(1)}, u32[]{:S(2)}, u32[]{:S(2)}) collective-permute-start(bf16[4,32,128]{2,1,0:T(8,128)(2,1)S(1)} %get-tuple-element.13), channel_id=1, source_target_pairs={{0,4},{2,6},{4,0},{6,2},{1,5},{3,7},{5,1},{7,3},{8,12},{10,14},{12... | collective-permute-start | bytes 98312 | tf_op jit(solution)/shard_map/ppermute | solution.py:327
  7.9 19.9 %all-to-all-start = ((bf16[32,9,2,128]{3,2,1,0:T(2,128)(2,1)}), bf16[32,9,2,128]{3,2,1,0:T(2,128)(2,1)S(1)}, u32[]{:S(2)}, u32[]{:S(2)}) async-start(bf16[32,9,2,128]{3,2,1,0:T(2,128)(2,1)} %bitcast.11), calls=%async_computation | async-start | bytes 294912 | tf_op jit(solution)/shard_map/all_to_all | solution.py:311
  18.0 0.7 %copy-start.2 = (f32[8]{0:T(128)S(1)}, f32[8]{0:T(128)}, u32[]{:S(2)}) copy-start(f32[8]{0:T(128)} %param.9) | copy-start | bytes 100
  18.1 0.7 %copy-start.1 = (s32[8,48]{1,0:T(8,128)S(1)}, s32[8,48]{1,0:T(8,128)}, u32[]{:S(2)}) copy-start(s32[8,48]{1,0:T(8,128)} %param.10) | copy-start | bytes 4612
  18.8 8.4 %collective-permute-start = (f32[136,128]{1,0:T(8,128)S(1)}, f32[136,128]{1,0:T(8,128)S(1)}, u32[]{:S(2)}, u32[]{:S(2)}) collective-permute-start(f32[136,128]{1,0:T(8,128)S(1)} %maximum_maximum_fusion), channel_id=1, source_target_pairs={{0,3},{1,2},{2,5},{3,4},{4,7},{5,6},{6,1},{7,0},{8,11},{9,10},{10,... | collective-permute-start | bytes 208904 | tf_op jit(solution)/shard_map/ppermute | solution.py:324
  21.5 5.8 %copy-start = (f32[32]{0:T(128)S(1)}, f32[32]{0:T(128)}, u32[]{:S(2)}) copy-start(f32[32]{0:T(128)} %param.8) | copy-start | bytes 388

commit v6 on v5

--- a/solution.py
+++ b/solution.py
@@ -16,6 +16,7 @@
 SLOTS = 48
 NESTS = 16
 HALF = 8
+WIDE = 24
 DRAWS = 512
 MARKETS = 1024
 LANES = 128
@@ -46,14 +47,23 @@
     return lax.dot_general(a, b, (((1,), (1,)), ((), ())), preferred_element_type=f32)
 
 
-def pack(f_hbm, l_hbm, out_hbm, f_ref, l_ref, g_ref, o_ref, out_ref, sems):
+def pack(f_hbm, l_hbm, taste_hbm, members_hbm, rate_hbm, out_hbm, both_ref, t0_ref, t2_ref, t3_ref,
+         f_ref, l_ref, taste_ref, members_ref, rate_ref, g_ref, o_ref, out_ref, sems):
     loads = [pltpu.make_async_copy(l_hbm, l_ref, sems.at[PARTS])]
     for c in range(PARTS):
         part = pl.ds(c * K // PARTS, K // PARTS)
         loads.append(pltpu.make_async_copy(f_hbm.at[part], f_ref.at[part], sems.at[c]))
+    d, n = lax.axis_index("draw"), lax.axis_index("nest")
+    first = lax.rem(d + 1, 4) * 8 + (1 - n) * QUAD
+    loads.append(pltpu.make_async_copy(taste_hbm.at[pl.ds(first, QUAD)], taste_ref, sems.at[PARTS + 1]))
+    loads.append(pltpu.make_async_copy(members_hbm, members_ref, sems.at[PARTS + 2]))
+    loads.append(pltpu.make_async_copy(rate_hbm, rate_ref, sems.at[PARTS + 3]))
+    for c, (shift, ref) in enumerate(((0, t0_ref), (2, t2_ref), (3, t3_ref))):
+        start = lax.rem(d + shift, 4) * 8 + n * QUAD
+        loads.append(pltpu.make_async_copy(taste_hbm.at[pl.ds(start, QUAD)], ref, sems.at[PARTS + 4 + c]))
     for load in loads:
         load.start()
-    base = (lax.axis_index("draw") * 2 + lax.axis_index("nest")) * QUAD
+    base = (d * 2 + n) * QUAD
     market = iota((MARKETS, LANES), 0)
     lane = iota((MARKETS, LANES), 1)
     pick = jnp.where(market == (lane % BLOCKS) * 32 + base + lane // BLOCKS, 1.0, 0.0).astype(bf16)
@@ -71,6 +81,17 @@
     second = jnp.concatenate([logs[2 * PROD :]] * QUAD + [jnp.zeros((64, LANES), f32)], axis=0)
     o_ref[pl.ds(PROD, BLOCKS, stride=ROWS), :] = dot_t(spread, jnp.where(own, first, 0.0).astype(bf16))
     o_ref[pl.ds(PROD + 1, BLOCKS, stride=ROWS), :] = dot_t(spread, jnp.where(own, second, 0.0).astype(bf16))
+
+    for load in loads[1 + PARTS : 4 + PARTS]:
+        load.wait()
+    both_ref[: QUAD * K, :] = taste_ref[...].astype(f32).reshape(QUAD * K, LANES)
+    both_ref[QUAD * K :, :] = jnp.zeros((HALF, LANES), f32)
+    both_ref[QUAD * K :, :SLOTS] = members_ref[...].astype(f32)
+    square = iota((HALF, HALF), 0) == iota((HALF, HALF), 1)
+    rates = jnp.where(square, jnp.broadcast_to(rate_ref[...], (HALF, HALF)), 0.0)
+    rates = jnp.broadcast_to(jnp.sum(rates, axis=1, keepdims=True), (HALF, LANES))
+    nests = jnp.where(iota((HALF, LANES), 1) == SLOTS, rates, both_ref[QUAD * K :, :])
+    both_ref[QUAD * K :, :] = nests
 
     rows = K * PROD // PARTS
     for c in range(PARTS):
@@ -92,8 +113,8 @@
         part = pl.ds(c * half, half)
         stores.append(pltpu.make_async_copy(out_ref.at[part], out_hbm.at[part], sems.at[c]))
         stores[-1].start()
-    for store in stores:
-        store.wait()
+    for copy in loads[4 + PARTS :] + stores:
+        copy.wait()
 
 
 def across(x):
@@ -102,7 +123,7 @@
 
 def arrange(near_ref, next_ref, scale_ref, table_ref, hot_ref, pick_ref, mask_ref):
     first = lax.axis_index("nest") == 0
-    near, far = near_ref[...], next_ref[QUAD * K :, :]
+    near, far = near_ref[QUAD * K :, :], next_ref[QUAD * K :, :]
     table = jnp.concatenate([jnp.where(first, near, far), jnp.where(first, far, near)], axis=0)
     row, lane = iota((NESTS, LANES), 0), iota((NESTS, LANES), 1)
     filled = jnp.where((lane < SLOTS) & (table >= 0.0), 1.0, 0.0)
@@ -238,7 +259,7 @@
             for x, y in zip(*tiles)
         ]
 
-    lag = 2
+    lag = 1
     for stage in range(ITERS * QUAD):
         q = stage % QUAD
         ahead = stage - lag if 0 <= stage - lag < (ITERS - 1) * QUAD else None
@@ -256,15 +277,21 @@
         ]
 
     ranks = table_ref[NESTS + K :, :]
+    whole_lane = iota((NESTS, LANES), 1)
+    finals = []
     for q in range(QUAD):
         final = jnp.zeros((NESTS, LANES), f32)
         for o in range(2):
             result = (target[q][o] - outside[q][:HALF]) + value[q][o] * (rate[o] * math.log(2.0))
             result = jnp.where(table[o] >= 0.0, result, 0.0)
-            result = jnp.where(narrow < SLOTS, result, pltpu.roll(share[q][o], 64, 1))
+            result = jnp.where(narrow < SLOTS, result, pltpu.roll(share[q][o], SLOTS, 1))
             for r in range(HALF):
                 one = jnp.broadcast_to(result[r : r + 1, :], (NESTS, LANES))
                 final = jnp.where(ranks == float(o * HALF + r), one, final)
+        finals.append(final)
+    for q in range(QUAD - 1):
+        last = pltpu.roll(finals[QUAD - 1], 96 - 32 * q, 1)
+        final = jnp.where(whole_lane < 2 * SLOTS, finals[q], last)
         for n in range(2):
             for d in range(4):
                 out_ref[2 * d + n, q * HALF : (q + 1) * HALF, :] = final[n * HALF : (n + 1) * HALF]
@@ -284,47 +311,54 @@
         solve(len(PLACES), *inputs, slot_ref, taste_ref, l_ref)
 
 
-def unpack(r_ref, value_ref, share_ref):
+def unpack(r_ref, value_ref, share_ref, rows_ref):
+    lane = iota((8, LANES), 1)
     for g in range(HALF):
-        part = r_ref[pl.ds(g, 32, stride=HALF), :]
+        parts = [r_ref[pl.ds(q * HALF + g, 8, stride=WIDE), :] for q in range(QUAD - 1)]
+        last = [pltpu.roll(x, 32 * (q + 1), 1) for q, x in enumerate(parts)]
+        parts.append(jnp.where(lane < 32, last[0], jnp.where(lane < 64, last[1], last[2])))
+        for q, part in enumerate(parts):
+            rows_ref[pl.ds(g * 32 + q, 8, stride=QUAD), :] = part
+        part = rows_ref[g * 32 : (g + 1) * 32, :]
         value_ref[:, g * SLOTS : (g + 1) * SLOTS] = part[:, :SLOTS]
-        share_ref[:, g * SLOTS : (g + 1) * SLOTS] = part[:, 64 : 64 + SLOTS]
+        share_ref[:, g * SLOTS : (g + 1) * SLOTS] = part[:, SLOTS : 2 * SLOTS]
 
 
 def shards(features, taste_draws, taste_scale, nest_param, members, log_share):
-    send = pl.pallas_call(
+    inputs = (features, log_share, taste_draws, members, nest_param.reshape(1, HALF))
+    tastes = jax.ShapeDtypeStruct((QUAD, K, LANES), bf16)
+    send, near, *tastes = pl.pallas_call(
         pack,
         name="pack",
-        out_shape=jax.ShapeDtypeStruct((BLOCKS * ROWS, LANES), bf16),
-        in_specs=[HBM, HBM],
-        out_specs=HBM,
+        out_shape=(
+            jax.ShapeDtypeStruct((BLOCKS * ROWS, LANES), bf16),
+            jax.ShapeDtypeStruct((QUAD * K + HALF, LANES), f32),
+            *[tastes] * 3,
+        ),
+        in_specs=[HBM] * 5,
+        out_specs=(HBM, VMEM, VMEM, VMEM, VMEM),
         scratch_shapes=[
             pltpu.VMEM((K, PROD, MARKETS), bf16),
             pltpu.VMEM((PROD, MARKETS), f32),
+            pltpu.VMEM((QUAD, K, LANES), bf16),
+            pltpu.VMEM((HALF, SLOTS), i32),
+            pltpu.VMEM((1, HALF), f32),
             pltpu.VMEM((K * PROD, LANES), f32),
             pltpu.VMEM((BLOCKS * ROWS, LANES), f32),
             pltpu.VMEM((BLOCKS * ROWS, LANES), bf16),
-            pltpu.SemaphoreType.DMA((PARTS + 1,)),
+            pltpu.SemaphoreType.DMA((PARTS + 7,)),
         ],
-    )(features, log_share)
+        compiler_params=pltpu.CompilerParams(vmem_limit_bytes=8 * MIB),
+    )(*(pltpu.with_memory_space_constraint(x, pltpu.HBM) for x in inputs))
     send = send.reshape(BLOCKS, ROWS // 2, 2, LANES)
     recv = lax.all_to_all(send, "mkt", split_axis=0, concat_axis=0, tiled=True)
     recv = recv.reshape(BLOCKS * ROWS, LANES)
 
-    d, n = lax.axis_index("draw"), lax.axis_index("nest")
-
-    def tastes(shift, nest):
-        return lax.dynamic_slice_in_dim(taste_draws, (d + shift) % 4 * 8 + nest * QUAD, QUAD, 0)
-
-    near = jnp.concatenate(
-        [members.astype(f32), nest_param[:, None], jnp.zeros((HALF, LANES - SLOTS - 1), f32)], axis=1
-    )
-    both = jnp.concatenate([tastes(1, 1 - n).astype(f32).reshape(QUAD * K, LANES), near], axis=0)
     ring = [(2 * i + j, (i + 1) % 4 * 2 + 1 - j) for i in range(4) for j in range(2)]
-    both = lax.ppermute(both, ("draw", "nest"), ring)
-    others = []
+    both = lax.ppermute(near, ("draw", "nest"), ring)
     for shift in (2, 3):
-        others.append(lax.ppermute(tastes(shift, n), "draw", [(i, (i + shift) % 4) for i in range(4)]))
+        ring = [(i, (i + shift) % 4) for i in range(4)]
+        tastes[shift - 1] = lax.ppermute(tastes[shift - 1], "draw", ring)
     rows = len(PLACES) * HALF
     plan = pl.pallas_call(
         arrange,
@@ -343,7 +377,7 @@
     results = pl.pallas_call(
         contract,
         name="contract",
-        out_shape=jax.ShapeDtypeStruct((8, 32, LANES), f32),
+        out_shape=jax.ShapeDtypeStruct((8, WIDE, LANES), f32),
         in_specs=[VMEM] * 9,
         out_specs=VMEM,
         scratch_shapes=[
@@ -352,7 +386,7 @@
             pltpu.VMEM((BLOCKS * ROWS, LANES), f32),
         ],
         compiler_params=pltpu.CompilerParams(vmem_limit_bytes=36 * MIB),
-    )(recv, tastes(0, n), both, *others, *plan)
+    )(recv, tastes[0], both, *tastes[1:], *plan)
     gathered = lax.all_to_all(results, ("draw", "nest"), split_axis=0, concat_axis=0, tiled=True)
     shape = jax.ShapeDtypeStruct((32, HALF * SLOTS), f32)
     return pl.pallas_call(
@@ -361,8 +395,9 @@
         out_shape=(shape, shape),
         in_specs=[VMEM],
         out_specs=(VMEM, VMEM),
+        scratch_shapes=[pltpu.VMEM((8 * 32, LANES), f32)],
         compiler_params=pltpu.CompilerParams(vmem_limit_bytes=2 * MIB),
-    )(gathered.reshape(256, LANES))
+    )(gathered.reshape(8 * WIDE, LANES))
 
 
 def solution(mesh):

time: 46.9 us -> 42.5 us (0.906)
  waiting for transfers between devices: 5.75 us -> 1.97 us
  local copies, waits for them, and re-layouts: 1.54 us -> 0.01 us
  starting transfers between devices: 16.4 us -> 17.6 us
    ppermute x3, waiting for transfers between devices: 5.75 us -> 1.97 us  [the longest x2 1.09 us: shards(): tastes[shift - 1] = lax.ppermute(tastes[shift - 1], 'draw', ring)]
    ppermute x3, starting transfers between devices: 6.27 us -> 7.46 us  [the longest x2 4.24 us: shards(): tastes[shift - 1] = lax.ppermute(tastes[shift - 1], 'draw', ring)]
    dynamic_slice x1 -> x0, local copies, waits for them, and re-layouts: 0.83 us -> none  [tastes(): lax.dynamic_slice_in_dim(taste_draws, (d + shift) % 4 * 8 + nest * QUAD,...]
    unnamed x6 -> x2, local copies, waits for them, and re-layouts: 0.63 us -> 0.01 us
  transfers between devices with their start and end apart: 4 -> 4, of which waited for: 1 -> 3; matrix products, arithmetic and copies ran while one was open for 1% -> 0% of each run, Pallas kernels for 7% -> 1%
where the time goes in v6:
time: 42.5 us; the launch traced here: 42.3 us
  starting transfers between devices  17.6 us (41%)
  blocking collectives  13.4 us (32%)
  Pallas kernels  8.66 us (20%)
  waiting for transfers between devices  1.97 us (5%)
  between operations  0.67 us (2%)
    all_to_all x1, blocking collectives, shards(): lax.all_to_all(results, ('draw', 'nest'), split_axis=0, concat_axis=0, ti...  13.4 us
    all_to_all x1, starting transfers between devices, shards(): recv = lax.all_to_all(send, 'mkt', split_axis=0, concat_axis=0, tiled=True)  10.1 us
    pallas_call x1, Pallas kernels, shards(): pl.pallas_call(contract, name='contract', out_shape=jax.ShapeDtypeStruct(...  4.41 us
    ppermute x2, starting transfers between devices, shards(): tastes[shift - 1] = lax.ppermute(tastes[shift - 1], 'draw', ring)  4.24 us
    ppermute x1, starting transfers between devices, shards(): both = lax.ppermute(near, ('draw', 'nest'), ring)  3.22 us
    pallas_call x1, Pallas kernels, shards(): pl.pallas_call(pack, name='pack', out_shape=(jax.ShapeDtypeStruct((BLOCKS...  2.82 us
    ppermute x2, waiting for transfers between devices, shards(): tastes[shift - 1] = lax.ppermute(tastes[shift - 1], 'draw', ring)  1.09 us
    ppermute x1, waiting for transfers between devices, shards(): both = lax.ppermute(near, ('draw', 'nest'), ring)  0.88 us
  transfers between devices with their start and end apart: 4, of which 3 were waited for; matrix products, arithmetic and copies ran while one was open for 0% of the time, Pallas kernels for 1%

profile of v6, /device:TPU:2, one launch (start us, length us, event | category | flops | bytes accessed | tf_op | source)
XLA Modules:
  0.0 42.3 jit_solution(13232791466609310583)
XLA Ops:
  0.6 2.8 %pack.1 = (bf16[576,128]{1,0:T(8,128)(2,1)}, f32[136,128]{1,0:T(8,128)S(1)}, bf16[4,32,128]{2,1,0:T(8,128)(2,1)S(1)}, bf16[4,32,128]{2,1,0:T(8,128)(2,1)S(1)}, bf16[4,32,128]{2,1,0:T(8,128)(2,1)S(1)}) custom-call(bf16[32,16,1024]{2,1,0:T(8,128)(2,1)} %f_hbm.1, f32[16,1024]{1,0:T(8,128)} %l_hbm.1, bf16[32,32,128]{2,1,0:T(8,128)(2,1)} %taste_hbm.1, ...), custom_call_target="tpu_custom_call" | custom-call | tf_op jit(solution)/shard_map/pack/pallas_call | solution.py:330
  3.5 10.1 %all-to-all-start = ((bf16[32,9,2,128]{3,2,1,0:T(2,128)(2,1)}), bf16[32,9,2,128]{3,2,1,0:T(2,128)(2,1)S(1)}, u32[]{:S(2)}, u32[]{:S(2)}) async-start(bf16[32,9,2,128]{3,2,1,0:T(2,128)(2,1)} %bitcast.1), calls=%async_computation | async-start | bytes 294912 | tf_op jit(solution)/shard_map/all_to_all | solution.py:354
  13.6 3.2 %collective-permute-start = (f32[136,128]{1,0:T(8,128)S(1)}, f32[136,128]{1,0:T(8,128)S(1)}, u32[]{:S(2)}, u32[]{:S(2)}) collective-permute-start(f32[136,128]{1,0:T(8,128)S(1)} %get-tuple-element.13.near_ref), channel_id=1, source_target_pairs={{0,3},{1,2},{2,5},{3,4},{4,7},{5,6},{6,1},{7,0},{8,11},{9,10},{10,... | collective-permute-start | bytes 208904 | tf_op jit(solution)/shard_map/ppermute | solution.py:358
  16.8 2.9 %collective-permute-start.1 = (bf16[4,32,128]{2,1,0:T(8,128)(2,1)S(1)}, bf16[4,32,128]{2,1,0:T(8,128)(2,1)S(1)}, u32[]{:S(2)}, u32[]{:S(2)}) collective-permute-start(bf16[4,32,128]{2,1,0:T(8,128)(2,1)S(1)} %get-tuple-element.14), channel_id=1, source_target_pairs={{0,4},{2,6},{4,0},{6,2},{1,5},{3,7},{5,1},{7,3},{8,12},{10,14},{12... | collective-permute-start | bytes 98312 | tf_op jit(solution)/shard_map/ppermute | solution.py:361
  19.7 0.0 copy-start
  19.7 1.3 %collective-permute-start.2 = (bf16[4,32,128]{2,1,0:T(8,128)(2,1)S(1)}, bf16[4,32,128]{2,1,0:T(8,128)(2,1)S(1)}, u32[]{:S(2)}, u32[]{:S(2)}) collective-permute-start(bf16[4,32,128]{2,1,0:T(8,128)(2,1)S(1)} %get-tuple-element.15), channel_id=1, source_target_pairs={{0,6},{2,0},{4,2},{6,4},{1,7},{3,1},{5,3},{7,5},{8,14},{10,8},{12,... | collective-permute-start | bytes 98312 | tf_op jit(solution)/shard_map/ppermute | solution.py:361
  21.0 0.9 %collective-permute-done.next_ref.t1_ref = f32[136,128]{1,0:T(8,128)S(1)} collective-permute-done((f32[136,128]{1,0:T(8,128)S(1)}, f32[136,128]{1,0:T(8,128)S(1)}, u32[]{:S(2)}, u32[]{:S(2)}) %collective-permute-start) | collective-permute-done | bytes 69664 | tf_op jit(solution)/shard_map/ppermute | solution.py:358
  21.9 0.0 copy-done
  21.9 0.6 %arrange.1 = (f32[64,128]{1,0:T(8,128)S(1)}, bf16[768,512]{1,0:T(8,128)(2,1)S(1)}, bf16[768,128]{1,0:T(8,128)(2,1)S(1)}, bf16[768,128]{1,0:T(8,128)(2,1)S(1)}) custom-call(f32[136,128]{1,0:T(8,128)S(1)} %get-tuple-element.13.near_ref, f32[136,128]{1,0:T(8,128)S(1)} %collective-permute-done.next_ref.t1_ref, f32[1,32]{1,0:T(1,128)S(1)} %bitcast.7), custom_call_target="tpu_custom_call" | custom-call | flops 2000000 | bytes 2000000 | tf_op jit(solution)/shard_map/arrange/pallas_call | solution.py:363
  22.5 0.3 collective-permute-done.1.t2_ref
  22.8 0.8 %collective-permute-done.2.t3_ref = bf16[4,32,128]{2,1,0:T(8,128)(2,1)S(1)} collective-permute-done((bf16[4,32,128]{2,1,0:T(8,128)(2,1)S(1)}, bf16[4,32,128]{2,1,0:T(8,128)(2,1)S(1)}, u32[]{:S(2)}, u32[]{:S(2)}) %collective-permute-start.2) | collective-permute-done | bytes 32800 | tf_op jit(solution)/shard_map/ppermute | solution.py:361
  23.6 0.0 all-to-all-done
  23.6 4.4 %contract.1 = f32[8,24,128]{2,1,0:T(8,128)S(1)} custom-call(bf16[576,128]{1,0:T(8,128)(2,1)S(1)} %bitcast.5, bf16[4,32,128]{2,1,0:T(8,128)(2,1)S(1)} %get-tuple-element.12.t0_ref, f32[136,128]{1,0:T(8,128)S(1)} %collective-permute-done.next_ref.t1_ref, bf16[4,32,128]{2,1,0:T(8,128)(2,1)S(1)} %collective-permute-done.1.t2_ref, ...), custom_call_target="tpu_custom_call" | custom-call | tf_op jit(solution)/shard_map/contract/pallas_call | solution.py:377
  28.0 13.4 %all_to_all.10 = f32[8,24,128]{2,1,0:T(8,128)S(1)} all-to-all(f32[8,24,128]{2,1,0:T(8,128)S(1)} %contract.1), channel_id=1, replica_groups=mesh['mkt'=32,'draw'=4,'nest'=2] {'draw','nest'}, dimensions={0} | all-to-all | bytes 196608 | tf_op jit(solution)/shard_map/all_to_all | solution.py:390
  41.4 0.8 %unpack.1 = (f32[32,384]{1,0:T(8,128)}, f32[32,384]{1,0:T(8,128)}) custom-call(f32[192,128]{1,0:T(8,128)S(1)} %bitcast.6), custom_call_target="tpu_custom_call" | custom-call | tf_op jit(solution)/shard_map/unpack/pallas_call | solution.py:392
Async XLA Ops:
  3.5 20.1 %all-to-all-start = ((bf16[32,9,2,128]{3,2,1,0:T(2,128)(2,1)}), bf16[32,9,2,128]{3,2,1,0:T(2,128)(2,1)S(1)}, u32[]{:S(2)}, u32[]{:S(2)}) async-start(bf16[32,9,2,128]{3,2,1,0:T(2,128)(2,1)} %bitcast.1), calls=%async_computation | async-start | bytes 294912 | tf_op jit(solution)/shard_map/all_to_all | solution.py:354
  13.6 8.3 %collective-permute-start = (f32[136,128]{1,0:T(8,128)S(1)}, f32[136,128]{1,0:T(8,128)S(1)}, u32[]{:S(2)}, u32[]{:S(2)}) collective-permute-start(f32[136,128]{1,0:T(8,128)S(1)} %get-tuple-element.13.near_ref), channel_id=1, source_target_pairs={{0,3},{1,2},{2,5},{3,4},{4,7},{5,6},{6,1},{7,0},{8,11},{9,10},{10,... | collective-permute-start | bytes 208904 | tf_op jit(solution)/shard_map/ppermute | solution.py:358
  16.8 6.0 %collective-permute-start.1 = (bf16[4,32,128]{2,1,0:T(8,128)(2,1)S(1)}, bf16[4,32,128]{2,1,0:T(8,128)(2,1)S(1)}, u32[]{:S(2)}, u32[]{:S(2)}) collective-permute-start(bf16[4,32,128]{2,1,0:T(8,128)(2,1)S(1)} %get-tuple-element.14), channel_id=1, source_target_pairs={{0,4},{2,6},{4,0},{6,2},{1,5},{3,7},{5,1},{7,3},{8,12},{10,14},{12... | collective-permute-start | bytes 98312 | tf_op jit(solution)/shard_map/ppermute | solution.py:361
  19.7 2.2 %copy-start = (f32[32]{0:T(128)S(1)}, f32[32]{0:T(128)}, u32[]{:S(2)}) copy-start(f32[32]{0:T(128)} %param.8) | copy-start | bytes 388
  19.7 3.9 %collective-permute-start.2 = (bf16[4,32,128]{2,1,0:T(8,128)(2,1)S(1)}, bf16[4,32,128]{2,1,0:T(8,128)(2,1)S(1)}, u32[]{:S(2)}, u32[]{:S(2)}) collective-permute-start(bf16[4,32,128]{2,1,0:T(8,128)(2,1)S(1)} %get-tuple-element.15), channel_id=1, source_target_pairs={{0,6},{2,0},{4,2},{6,4},{1,7},{3,1},{5,3},{7,5},{8,14},{10,8},{12,... | collective-permute-start | bytes 98312 | tf_op jit(solution)/shard_map/ppermute | solution.py:361
